TPU v7x, 256 devices: a 2x2x32 block of a 4x8x32 slice. The times are simulated.
256 devices in a mesh: parts: 4 (over x, y), env: 64 (over z, core).
Axes of the slice: x: 2, y: 2, z: 32, core: 2. Of those that a mesh axis runs over, the one named last changes fastest.
The devices are a block of a 4x8x32 slice.
Arguments:
- first_obs: float32 [48, 32768], P(None, ('parts', 'env')), parts along dimension 1, may hold values from -6 to 6
- dyn_state: float32 [48, 48], replicated, may hold values from -0.875 to 0.875
- dyn_act: float32 [48, 12], replicated, may hold values from -1.75 to 1.75
- contact_gain: float32 [4, 48, 48], replicated, may hold values from -0.875 to 0.875
- reward_weight: float32 [48], replicated, may hold values from 0.1 to 1
- contacts: int32 [8, 4, 32768], P(None, None, ('parts', 'env')), parts along dimension 2, may hold values 0 or 1
- action_noise: int32 [8, 12, 32768], P(None, None, ('parts', 'env')), parts along dimension 2, may hold values from -32768 to 32767
- policy_in: bfloat16 [512, 48], replicated, may hold values from -0.875 to 0.875
- policy_out: bfloat16 [12, 512], replicated, may hold values from -0.25 to 0.25
- critic_in: bfloat16 [48, 1024], replicated, may hold values from -0.875 to 0.875
- critic_middle: bfloat16 [1024, 1024], replicated, may hold values from -0.1875 to 0.1875
- critic_out: bfloat16 [1024], replicated, may hold values from -0.1875 to 0.1875
Outputs:
- td_targets: float32 [8, 32768], P(None, ('parts', 'env')), parts along dimension 1
- grad_middle: float32 [4096, 1024], P(('parts', 'env')), parts along dimension 0
- grad_in: float32 [192, 1024], P('parts'), parts along dimension 0
- grad_out: float32 [4096], P('parts'), parts along dimension 0
There are 4 independent parts, one for each index of `parts`. A program takes and returns all parts, laid end to end along the dimension named above; an argument that names none is the same for every part. Nothing has to cross between parts.
Inputs may be any that keep to these rules, and one draw needn't show every extreme that they name: `contacts`: 1 where the foot is in contact. `action_noise`: noise in units of 0.3 / 32768.
All inputs are finite; a program needn't handle non-finite values. No bound on the sum of `contacts` on one device may be relied on, other than what follows from the above.
Results may differ from a plain program's by a relative error of at most 0.018.
Values sent between devices are 32-bit elements; how exact they have to be, the bound alone decides.
No kernel may reach another device: no remote copies, remote signals or barrier semaphores. Data moves between devices by JAX's collectives and lax.ppermute only.
A program may use at most 64 MiB of HBM per device.

v0:
```python
import functools
import math

import jax
import jax.numpy as jnp
import numpy as np
from jax import lax
from jax.experimental import pallas as pl
from jax.experimental.pallas import tpu as pltpu
from jax.sharding import PartitionSpec as P


TIME_STEP = 0.05
NOISE_UNIT = 0.3 / 32768.0
DISCOUNT = 0.99
TRACE_DECAY = 0.95
LEVELS = 2
CORES = 2

F32 = jnp.float32
BF16 = jnp.bfloat16
NT = (((1,), (1,)), ((), ()))
TN = (((0,), (0,)), ((), ()))


def mm(a, b, dims=(((1,), (0,)), ((), ()))):
    return lax.dot_general(a, b, dims, preferred_element_type=F32)


def message_orders(ring):
    d = 2**LEVELS
    half = ring // 2
    behind = [-o for o in range(d, half + 1, d)]
    ahead = list(range(half, 0, -d))
    orders = [behind[:-1] + ahead + [0]]
    for level in reversed(range(LEVELS)):
        d = 2**level
        right, left = [o + d for o in behind], [o - d for o in ahead]
        orders = [right, left] + orders
        behind, ahead = right + behind, left + ahead
    return orders


def column(row, lanes):
    return jnp.transpose(jnp.broadcast_to(row, (lanes, row.shape[1])))


def spread_gradient(slot_ref, first, delta, odd, mine_ref, yours_ref):
    cores = CORES
    count, depth, _ = mine_ref.shape
    rows = delta.shape[1]
    index = lax.axis_index("env")
    here, core = index // cores, lax.rem(index, cores)
    parity = lax.rem(here + odd, 2)
    size = cores * depth
    per = 256 // size
    for m in range(count // per):
        owners = [2 * (m * per + i) + parity for i in range(per)]
        left = jnp.concatenate(
            [first[pl.ds(pl.multiple_of(o * size, size), size), :rows] for o in owners], axis=0
        )
        part = mm(left, delta[...], NT)
        for i, owner in enumerate(owners):
            slot = slot_ref[lax.rem(owner - here + 2 * count, 2 * count)]
            low = part[i * size : i * size + depth]
            high = part[i * size + depth : (i + 1) * size]
            mine_ref[slot] = jnp.where(core == 0, low, high)
            yours_ref[slot] = jnp.where(core == 0, high, low)


def window_kernel(
    loss_scale,
    slot_ref,
    obs_ref,
    dyn_state_ref,
    dyn_act_ref,
    gain_ref,
    reward_weight_ref,
    contacts_ref,
    noise_ref,
    policy_in_ref,
    policy_out_ref,
    critic_in_ref,
    critic_middle_ref,
    critic_out_ref,
    targets_ref,
    inputs,
    first,
    middle,
    delta,
    weight_rows,
    mine_ref,
    yours_ref,
    state_mix,
    middle_copy,
    middle_t,
    out_col,
    act_cols,
    weight_col,
    arrived,
):
    fetch = pltpu.make_async_copy(critic_middle_ref, middle_copy, arrived)
    fetch.start()
    obs, env = obs_ref.shape
    steps, feet, _ = contacts_ref.shape
    act = dyn_act_ref.shape[0]
    pol = policy_out_ref.shape[1]
    hid = critic_middle_ref.shape[0]
    rows = steps * env
    mixing = jnp.concatenate(
        [jnp.transpose(policy_in_ref[...].astype(F32)), dyn_state_ref[...]]
        + [gain_ref[k] for k in range(feet)],
        axis=0,
    )
    top = mixing.astype(BF16).astype(F32)
    state_mix[...] = jnp.concatenate([top, top, mixing - top], axis=1).astype(BF16)
    for a in range(act):
        act_cols[a] = column(dyn_act_ref[a : a + 1, :], env)
    weight_col[...] = column(reward_weight_ref[...], env)
    heads = critic_out_ref[...].astype(F32)
    for j in range(hid // env):
        out_col[j * env : (j + 1) * env, :] = column(heads[j : j + 1, :], env)

    state = obs_ref[...]
    rewards = []
    for t in range(steps):
        high = state.astype(BF16)
        low = (state - high.astype(F32)).astype(BF16)
        inputs[:, t * env : (t + 1) * env] = high
        mixed = mm(state_mix[...], jnp.concatenate([high, low, high], axis=0))
        hidden = jnp.tanh(mixed[:pol]).astype(BF16)
        noise = noise_ref[:, t, :].astype(F32)
        action = jnp.tanh(mm(policy_out_ref[...], hidden)) + NOISE_UNIT * noise
        drift = jnp.tanh(mixed[pol : pol + obs])
        for k in range(feet):
            start = pol + obs * (k + 1)
            touching = contacts_ref[t, k : k + 1, :].astype(F32)
            drift = drift - mixed[start : start + obs] * touching
        for a in range(act):
            drift = drift + act_cols[a] * action[a : a + 1, :]
        state = state + TIME_STEP * drift
        rewards.append(
            0.5
            - jnp.sum(weight_col[...] * state * state, axis=0, keepdims=True) / obs
            - 0.1 * (jnp.sum(action * action, axis=0, keepdims=True) / act)
        )
    inputs[:, rows:] = state.astype(BF16)
    fetch.wait()
    middle_t[...] = jnp.transpose(middle_copy[...])

    block = 256
    for m in range(hid // block):
        at = slice(m * block, (m + 1) * block)
        pre = mm(critic_in_ref[:, at], inputs[...], TN)
        first[at, :] = jnp.maximum(pre, 0.0).astype(BF16)
    values = jnp.zeros((8, rows + env), F32)
    out_row = jnp.concatenate([heads[j : j + 1, :] for j in range(hid // env)], axis=1)
    out_row = jnp.broadcast_to(out_row, (8, hid)).astype(BF16)
    for m in range(hid // block):
        at = slice(m * block, (m + 1) * block)
        kept = jnp.maximum(mm(middle_t[at, :], first[...]), 0.0).astype(BF16)
        middle[at, :] = kept
        values = values + mm(out_row[:, at], kept)
    value = [values[0:1, t * env : (t + 1) * env] for t in range(steps + 1)]
    target = value[steps]
    weights = [None] * steps
    for t in reversed(range(steps)):
        target = rewards[t] + DISCOUNT * (
            (1.0 - TRACE_DECAY) * value[t + 1] + TRACE_DECAY * target
        )
        targets_ref[t : t + 1, :] = target
        weights[t] = loss_scale * (value[t] - target)
        weight_rows[t : t + 1, :] = weights[t]
    for t in range(steps):
        lanes = slice(t * env, (t + 1) * env)
        scaled = out_col[...] * weights[t]
        delta[:, lanes] = jnp.where(middle[:, lanes] > 0, scaled, 0.0).astype(BF16)

    spread_gradient(slot_ref, first, delta, 1, mine_ref, yours_ref)


def even_kernel(slot_ref, first, delta, mine_ref, yours_ref):
    spread_gradient(slot_ref, first, delta, 0, mine_ref, yours_ref)


def back_kernel(
    critic_middle_ref, inputs, first, middle, delta, weight_rows, small_ref, first_delta
):
    obs = inputs.shape[0]
    hid, rows = delta.shape
    steps = weight_rows.shape[0]
    block = 256
    for m in range(hid // block):
        at = slice(m * block, (m + 1) * block)
        back = mm(critic_middle_ref[at, :], delta[...])
        first_delta[at, :] = jnp.where(first[at, :rows] > 0, back, 0.0).astype(BF16)
    small_ref[...] = jnp.zeros_like(small_ref)
    small_ref[:obs, :] = mm(inputs[:, :rows], first_delta[...], NT)
    weight_row = jnp.concatenate([weight_rows[t : t + 1, :] for t in range(steps)], axis=1)
    weight_high = weight_row.astype(BF16)
    weight_low = (weight_row - weight_high.astype(F32)).astype(BF16)
    both = mm(jnp.concatenate([weight_high, weight_low], axis=0), middle[:, :rows], NT)
    small_ref[obs : obs + 1, :] = both[0:1] + both[1:2]


def local_window(args, devices, orders):
    (first_obs, dyn_state, dyn_act, contact_gain, reward_weight, contacts, action_noise,
     policy_in, policy_out, critic_in, critic_middle, critic_out) = args
    obs, env = first_obs.shape
    steps, feet = contacts.shape[:2]
    hid = critic_middle.shape[0]
    pol = policy_out.shape[1]
    rows = steps * env
    act = dyn_act.shape[1]
    loss_scale = math.sqrt(hid) / (rows * devices)
    depth = hid // devices
    ring = devices // CORES
    half = ring // 2
    slots = np.zeros((ring,), np.int32)
    for slot, offset in enumerate(sum(orders, [])):
        slots[offset % ring] = slot % half
    slots = jnp.asarray(slots)
    vmem = pl.BlockSpec(memory_space=pltpu.VMEM)
    smem = pl.BlockSpec(memory_space=pltpu.SMEM)
    anywhere = pl.BlockSpec(memory_space=pl.ANY)
    sent = pltpu.VMEM((half, depth, hid), F32)

    def far(x):
        return pltpu.with_memory_space_constraint(x, pltpu.MemorySpace.HBM)

    targets, inputs, first, middle, delta, weight_rows, *odd = pl.pallas_call(
        functools.partial(window_kernel, loss_scale),
        in_specs=[smem] + [vmem] * 10 + [anywhere, vmem],
        out_specs=[vmem] * 8,
        out_shape=[
            jax.ShapeDtypeStruct((steps, env), F32),
            pltpu.VMEM((obs, rows + env), BF16),
            pltpu.VMEM((hid, rows + env), BF16),
            pltpu.VMEM((hid, rows + env), BF16),
            pltpu.VMEM((hid, rows), BF16),
            pltpu.VMEM((steps, env), F32),
            sent,
            sent,
        ],
        scratch_shapes=[
            pltpu.VMEM((pol + obs * (feet + 1), 3 * obs), BF16),
            pltpu.VMEM((hid, hid), BF16),
            pltpu.VMEM((hid, hid), BF16),
            pltpu.VMEM((hid, env), F32),
            pltpu.VMEM((act, obs, env), F32),
            pltpu.VMEM((obs, env), F32),
            pltpu.SemaphoreType.DMA(()),
        ],
        compiler_params=pltpu.CompilerParams(vmem_limit_bytes=24 * 2**20),
    )(
        *(
            far(x)
            for x in (
                slots, first_obs, dyn_state, dyn_act.T, contact_gain, reward_weight[None, :],
                contacts, action_noise.transpose(1, 0, 2), policy_in.T, policy_out, critic_in,
                critic_middle, critic_out.reshape(-1, env),
            )
        )
    )

    even = pl.pallas_call(
        even_kernel,
        in_specs=[smem, vmem, vmem],
        out_specs=[vmem] * 2,
        out_shape=[sent] * 2,
        compiler_params=pltpu.CompilerParams(vmem_limit_bytes=8 * 2**20),
        cost_estimate=pl.CostEstimate(flops=rows * hid * hid, bytes_accessed=0, transcendentals=0),
    )(far(slots), first, delta)

    def small_gradients(after, small_rows):
        tied = lax.optimization_barrier((weight_rows, after))
        small = pl.pallas_call(
            back_kernel,
            in_specs=[vmem] * 6,
            out_specs=vmem,
            out_shape=pltpu.VMEM((small_rows, hid), F32),
            scratch_shapes=[pltpu.VMEM((hid, rows), BF16)],
            compiler_params=pltpu.CompilerParams(vmem_limit_bytes=12 * 2**20),
            cost_estimate=pl.CostEstimate(
                flops=2 * rows * hid * (hid + 2 * obs), bytes_accessed=0, transcendentals=0
            ),
        )(critic_middle, inputs, first, middle, delta, tied[0])
        return small, tied[1]

    return targets, odd, even, small_gradients


def reduced_window(*args):
    devices = lax.axis_size("env")
    ring = devices // CORES
    index = lax.axis_index("env")
    obs = args[0].shape[0]
    hid = args[10].shape[0]
    depth = hid // devices
    small_rows = 8 * CORES * 2**LEVELS
    orders = message_orders(ring)

    bits = [2**k for k in range(LEVELS + 1)]
    held = lax.optimization_barrier((args[0], *(lax.bitwise_and(index, b) != 0 for b in bits)))
    args = (held[0],) + args[1:]
    flags = dict(zip(bits, held[1:]))
    targets, odd, even, small_gradients = local_window(args, devices, orders)

    def shift(x, d):
        pairs = [
            (z * CORES + c, (z + d) % ring * CORES + c) for z in range(ring) for c in range(CORES)
        ]
        return lax.ppermute(x, "env", pairs)

    def swap(x, mask):
        return lax.ppermute(x, "env", [(e, e ^ mask) for e in range(devices)])

    def halves(x, bit):
        half = x.shape[0] // 2
        low, high = x[:half], x[half:]
        return jnp.where(flags[bit], high, low), jnp.where(flags[bit], low, high)

    def joined(mine, other, bit):
        low, high = jnp.where(flags[bit], other, mine), jnp.where(flags[bit], mine, other)
        return jnp.concatenate([low, high], axis=0)

    sizes = [len(o) for o in orders]
    right, left = sizes[0], sizes[0] + sizes[1]
    total = odd[0] + swap(odd[1], 1)
    given = swap(even[1], 1)
    small, total = small_gradients(total, small_rows)
    messages = [total[:right].reshape(-1, hid), total[right:left].reshape(-1, hid)]
    for level in range(LEVELS):
        d = 2**level
        bit = CORES * d
        if level == 0:
            right = shift(messages[0], d)
            left = shift(messages[1], -d)
            right, left, given = lax.optimization_barrier((right, left, given))
            total = (even[0] + given).reshape(-1, hid)
            bounds = np.cumsum([0] + [s * depth for s in sizes[2:]])
            later = [total[a:b] for a, b in zip(bounds[:-1], bounds[1:])]
            kept, given = halves(small, 1)
            small = kept + swap(given, 1)
            kept, given = halves(small, bit)
            small = kept + swap(given, bit)
        else:
            kept, given = halves(small, bit)
            right, left, given = lax.optimization_barrier(
                (shift(messages[0], d), shift(messages[1], -d), swap(given, bit))
            )
            small = kept + given
        at = 0
        for k in range(0, len(later) - 1, 2):
            part = later[k].shape[0]
            later[k] = later[k] + right[at : at + part]
            later[k + 1] = later[k + 1] + left[at : at + part]
            at += part
        right, left = right[at:], left[at:]
        size = right.shape[0]
        pads = later[-1].shape[0] - size
        skip = size - depth
        later[-1] = (
            later[-1]
            + jnp.pad(right, ((0, pads), (0, 0)))
            + jnp.pad(left, ((skip, pads - skip), (0, 0)))
        )
        messages, later = later[:2], later[2:]

    (rest,) = messages
    d = 2**LEVELS
    hops = ring // (2 * d)
    own = small
    sums = {o: rest[k * depth : (k + 1) * depth] for k, o in enumerate(orders[-1])}
    right = jnp.concatenate([sums[hops * d], own], axis=0)
    left = jnp.concatenate([sums[-(hops - 1) * d], own], axis=0)
    for k in range(1, hops + 1):
        right = shift(right, d)
        if k < hops:
            left = shift(left, -d)
        right, left = lax.optimization_barrier((right, left))
        if k < hops:
            right = right + jnp.concatenate([sums[(hops - k) * d], own], axis=0)
        if k < hops - 1:
            left = left + jnp.concatenate([sums[-(hops - 1 - k) * d], own], axis=0)
    grad_middle = right[:depth] + left[:depth] + sums[0]
    small = right[depth:] + left[depth:] + own

    masks = range(1, 2**LEVELS)
    got = [small] + list(lax.optimization_barrier(tuple(swap(small, CORES * m) for m in masks)))
    for level in reversed(range(LEVELS)):
        got = [joined(got[m], got[m + 2**level], CORES * 2**level) for m in range(2**level)]
    small = joined(got[0], swap(got[0], 1), 1)
    return targets, grad_middle, small[:obs], small[obs]


def solution(mesh):
    split = ("parts", "env")
    return jax.shard_map(
        reduced_window,
        mesh=mesh,
        in_specs=(
            P(None, split),
            P(),
            P(),
            P(),
            P(),
            P(None, None, split),
            P(None, None, split),
            P(),
            P(),
            P(),
            P(),
            P(),
        ),
        out_specs=(P(None, split), P(split, None), P("parts", None), P("parts")),
        check_vma=False,
    )
```

profile of v0, /device:TPU:47, one launch (start us, length us, event | category | flops | bytes accessed | tf_op | source)
XLA Modules:
  0.0 136.4 jit_solution(17101829916019370223)
XLA Ops:
  0.6 10.8 %shard_map.156 = (f32[8,128]{1,0:T(8,128)}, bf16[48,1152]{1,0:T(8,128)(2,1)S(1)}, bf16[1024,1152]{1,0:T(8,128)(2,1)S(1)}, bf16[1024,1152]{1,0:T(8,128)(2,1)S(1)}...) custom-call(s32[32]{0:T(128)} %constant.16.clone.slot_ref, ...), custom_call_target="tpu_custom_call" | custom-call | tf_op jit(solution)/shard_map/pallas_call | solution.py:231
  11.4 0.7 collective-permute-start
  12.2 2.0 %shard_map.157 = (f32[16,16,1024]{2,1,0:T(8,128)S(1)}, f32[16,16,1024]{2,1,0:T(8,128)S(1)}) custom-call(s32[32]{0:T(128)} %constant.16.clone.slot_ref, bf16[1024,1152]{1,0:T(8,128)(2,1)S(1)} %get-tuple-element.39.first, bf16[1024,1024]{1,0:T(8,128)(2,1)S(1)} %get-tuple-element.40.delta), custom_call_target="tpu_custom_call" | custom-call | flops 1073741824 | tf_op jit(solution)/shard_map/pallas_call | solution.py:266
  14.1 0.0 copy-start
  14.2 0.3 collective-permute-start.3
  14.5 0.0 collective-permute-done
  14.5 0.2 add.68
  14.7 1.1 copy-done
  15.7 3.5 %shard_map.158 = f32[64,1024]{1,0:T(8,128)S(1)} custom-call(bf16[1024,1024]{1,0:T(8,128)(2,1)S(1)} %copy-done, bf16[48,1152]{1,0:T(8,128)(2,1)S(1)} %get-tuple-element.53.inputs, bf16[1024,1152]{1,0:T(8,128)(2,1)S(1)} %get-tuple-element.39.first, bf16[1024,1152]{1,0:T(8,128)(2,1)S(1)} %get-tuple-element.54.middle, ...), custom_call_target="tpu_custom_call" | custom-call | flops 2348810240 | tf_op jit(solution)/shard_map/pallas_call | solution.py:277
  19.3 0.1 collective-permute-start.6
  19.5 0.1 fusion.11
  19.6 2.0 %collective-permute-start.1 = (f32[128,1024]{1,0:T(8,128)S(1)}, f32[128,1024]{1,0:T(8,128)S(1)}, u32[]{:S(2)}, u32[]{:S(2)}) collective-permute-start(f32[128,1024]{1,0:T(8,128)S(1)} %bitcast.21), channel_id=1, source_target_pairs={{0,2},{1,3},{2,4},{3,5},{4,6},{5,7},{6,8},{7,9},{8,10},{9,11},{10,... | collective-permute-start | bytes 1572872 | tf_op jit(solution)/shard_map/ppermute | solution.py:313
  21.5 21.0 %collective-permute-start.2 = (f32[128,1024]{1,0:T(8,128)S(1)}, f32[128,1024]{1,0:T(8,128)S(1)}, u32[]{:S(2)}, u32[]{:S(2)}) collective-permute-start(f32[128,1024]{1,0:T(8,128)S(1)} %bitcast.20), channel_id=1, source_target_pairs={{0,62},{1,63},{2,0},{3,1},{4,2},{5,3},{6,4},{7,5},{8,6},{9,7},{10,... | collective-permute-start | bytes 1572872 | tf_op jit(solution)/shard_map/ppermute | solution.py:313
  42.6 0.0 collective-permute-done.6
  42.6 0.1 collective-permute-start.7
  42.8 0.0 collective-permute-done.3
  42.8 11.5 %collective-permute-done.1 = f32[128,1024]{1,0:T(8,128)S(1)} collective-permute-done((f32[128,1024]{1,0:T(8,128)S(1)}, f32[128,1024]{1,0:T(8,128)S(1)}, u32[]{:S(2)}, u32[]{:S(2)}) %collective-permute-start.1) | collective-permute-done | bytes 524320 | tf_op jit(solution)/shard_map/ppermute | solution.py:313
  54.3 0.0 collective-permute-done.2
  54.3 0.2 add.69
  54.5 0.1 fusion.13
  54.6 0.1 collective-permute-start.4
  54.7 0.1 fusion.14
  54.8 3.7 %collective-permute-start.5 = (f32[64,1024]{1,0:T(8,128)S(1)}, f32[64,1024]{1,0:T(8,128)S(1)}, u32[]{:S(2)}, u32[]{:S(2)}) collective-permute-start(f32[64,1024]{1,0:T(8,128)S(1)} %get-tuple-element.84), channel_id=1, source_target_pairs={{0,60},{1,61},{2,62},{3,63},{4,0},{5,1},{6,2},{7,3},{8,4},{9,5},{1... | collective-permute-start | bytes 786440 | tf_op jit(solution)/shard_map/ppermute | solution.py:313
  58.4 0.0 collective-permute-done.7
  58.5 0.1 collective-permute-start.8
  58.7 6.7 %collective-permute-done.8 = f32[8,1024]{1,0:T(8,128)S(1)} collective-permute-done((f32[8,1024]{1,0:T(8,128)S(1)}, f32[8,1024]{1,0:T(8,128)S(1)}, u32[]{:S(2)}, u32[]{:S(2)}) %collective-permute-start.8) | collective-permute-done | bytes 32800 | tf_op jit(solution)/shard_map/ppermute | solution.py:316
  65.4 0.3 collective-permute-done.4
  65.7 0.0 collective-permute-done.5
  65.7 0.1 fusion.2
  65.9 3.2 %collective-permute-start.10 = (f32[24,1024]{1,0:T(8,128)S(1)}, f32[24,1024]{1,0:T(8,128)S(1)}, u32[]{:S(2)}, u32[]{:S(2)}) collective-permute-start(f32[24,1024]{1,0:T(8,128)S(1)} %get-tuple-element.97), channel_id=1, source_target_pairs={{0,56},{1,57},{2,58},{3,59},{4,60},{5,61},{6,62},{7,63},{8,0},{9,1... | collective-permute-start | bytes 294920 | tf_op jit(solution)/shard_map/ppermute | solution.py:313
  69.1 2.3 %collective-permute-start.9 = (f32[24,1024]{1,0:T(8,128)S(1)}, f32[24,1024]{1,0:T(8,128)S(1)}, u32[]{:S(2)}, u32[]{:S(2)}) collective-permute-start(f32[24,1024]{1,0:T(8,128)S(1)} %get-tuple-element.98), channel_id=1, source_target_pairs={{0,8},{1,9},{2,10},{3,11},{4,12},{5,13},{6,14},{7,15},{8,16},{9,17... | collective-permute-start | bytes 294920 | tf_op jit(solution)/shard_map/ppermute | solution.py:313
  71.4 2.8 %collective-permute-done.10 = f32[24,1024]{1,0:T(8,128)S(1)} collective-permute-done((f32[24,1024]{1,0:T(8,128)S(1)}, f32[24,1024]{1,0:T(8,128)S(1)}, u32[]{:S(2)}, u32[]{:S(2)}) %collective-permute-start.10) | collective-permute-done | bytes 98336 | tf_op jit(solution)/shard_map/ppermute | solution.py:313
  74.2 2.5 %collective-permute-done.9 = f32[24,1024]{1,0:T(8,128)S(1)} collective-permute-done((f32[24,1024]{1,0:T(8,128)S(1)}, f32[24,1024]{1,0:T(8,128)S(1)}, u32[]{:S(2)}, u32[]{:S(2)}) %collective-permute-start.9) | collective-permute-done | bytes 98336 | tf_op jit(solution)/shard_map/ppermute | solution.py:313
  76.8 3.5 %collective-permute-start.12 = (f32[24,1024]{1,0:T(8,128)S(1)}, f32[24,1024]{1,0:T(8,128)S(1)}, u32[]{:S(2)}, u32[]{:S(2)}) collective-permute-start(f32[24,1024]{1,0:T(8,128)S(1)} %get-tuple-element.95), channel_id=1, source_target_pairs={{0,56},{1,57},{2,58},{3,59},{4,60},{5,61},{6,62},{7,63},{8,0},{9,1... | collective-permute-start | bytes 294920 | tf_op jit(solution)/shard_map/ppermute | solution.py:313
  80.3 2.0 %collective-permute-start.11 = (f32[24,1024]{1,0:T(8,128)S(1)}, f32[24,1024]{1,0:T(8,128)S(1)}, u32[]{:S(2)}, u32[]{:S(2)}) collective-permute-start(f32[24,1024]{1,0:T(8,128)S(1)} %get-tuple-element.96), channel_id=1, source_target_pairs={{0,8},{1,9},{2,10},{3,11},{4,12},{5,13},{6,14},{7,15},{8,16},{9,17... | collective-permute-start | bytes 294920 | tf_op jit(solution)/shard_map/ppermute | solution.py:313
  82.3 3.2 %collective-permute-done.12 = f32[24,1024]{1,0:T(8,128)S(1)} collective-permute-done((f32[24,1024]{1,0:T(8,128)S(1)}, f32[24,1024]{1,0:T(8,128)S(1)}, u32[]{:S(2)}, u32[]{:S(2)}) %collective-permute-start.12) | collective-permute-done | bytes 98336 | tf_op jit(solution)/shard_map/ppermute | solution.py:313
  85.4 3.3 %collective-permute-done.11 = f32[24,1024]{1,0:T(8,128)S(1)} collective-permute-done((f32[24,1024]{1,0:T(8,128)S(1)}, f32[24,1024]{1,0:T(8,128)S(1)}, u32[]{:S(2)}, u32[]{:S(2)}) %collective-permute-start.11) | collective-permute-done | bytes 98336 | tf_op jit(solution)/shard_map/ppermute | solution.py:313
  88.8 3.8 %collective-permute-start.14 = (f32[24,1024]{1,0:T(8,128)S(1)}, f32[24,1024]{1,0:T(8,128)S(1)}, u32[]{:S(2)}, u32[]{:S(2)}) collective-permute-start(f32[24,1024]{1,0:T(8,128)S(1)} %get-tuple-element.93), channel_id=1, source_target_pairs={{0,56},{1,57},{2,58},{3,59},{4,60},{5,61},{6,62},{7,63},{8,0},{9,1... | collective-permute-start | bytes 294920 | tf_op jit(solution)/shard_map/ppermute | solution.py:313
  92.6 1.9 %collective-permute-start.13 = (f32[24,1024]{1,0:T(8,128)S(1)}, f32[24,1024]{1,0:T(8,128)S(1)}, u32[]{:S(2)}, u32[]{:S(2)}) collective-permute-start(f32[24,1024]{1,0:T(8,128)S(1)} %get-tuple-element.94), channel_id=1, source_target_pairs={{0,8},{1,9},{2,10},{3,11},{4,12},{5,13},{6,14},{7,15},{8,16},{9,17... | collective-permute-start | bytes 294920 | tf_op jit(solution)/shard_map/ppermute | solution.py:313
  94.5 3.3 %collective-permute-done.14 = f32[24,1024]{1,0:T(8,128)S(1)} collective-permute-done((f32[24,1024]{1,0:T(8,128)S(1)}, f32[24,1024]{1,0:T(8,128)S(1)}, u32[]{:S(2)}, u32[]{:S(2)}) %collective-permute-start.14) | collective-permute-done | bytes 98336 | tf_op jit(solution)/shard_map/ppermute | solution.py:313
  97.8 5.2 %collective-permute-done.13 = f32[24,1024]{1,0:T(8,128)S(1)} collective-permute-done((f32[24,1024]{1,0:T(8,128)S(1)}, f32[24,1024]{1,0:T(8,128)S(1)}, u32[]{:S(2)}, u32[]{:S(2)}) %collective-permute-start.13) | collective-permute-done | bytes 98336 | tf_op jit(solution)/shard_map/ppermute | solution.py:313
  103.0 2.3 %collective-permute-start.15 = (f32[24,1024]{1,0:T(8,128)S(1)}, f32[24,1024]{1,0:T(8,128)S(1)}, u32[]{:S(2)}, u32[]{:S(2)}) collective-permute-start(f32[24,1024]{1,0:T(8,128)S(1)} %fusion.7), channel_id=1, source_target_pairs={{0,8},{1,9},{2,10},{3,11},{4,12},{5,13},{6,14},{7,15},{8,16},{9,17... | collective-permute-start | bytes 294920 | tf_op jit(solution)/shard_map/ppermute | solution.py:313
  105.3 8.3 %collective-permute-done.15 = f32[24,1024]{1,0:T(8,128)S(1)} collective-permute-done((f32[24,1024]{1,0:T(8,128)S(1)}, f32[24,1024]{1,0:T(8,128)S(1)}, u32[]{:S(2)}, u32[]{:S(2)}) %collective-permute-start.15) | collective-permute-done | bytes 98336 | tf_op jit(solution)/shard_map/ppermute | solution.py:313
  113.6 10.5 %collective-permute-start.18 = (f32[8,1024]{1,0:T(8,128)S(1)}, f32[8,1024]{1,0:T(8,128)S(1)}, u32[]{:S(2)}, u32[]{:S(2)}) collective-permute-start(f32[8,1024]{1,0:T(8,128)S(1)} %add_add_fusion), channel_id=1, source_target_pairs={{0,6},{1,7},{2,4},{3,5},{4,2},{5,3},{6,0},{7,1},{8,14},{9,15},{10,... | collective-permute-start | bytes 98312 | tf_op jit(solution)/shard_map/ppermute | solution.py:316
  124.1 0.0 collective-permute-start.17
  124.1 0.4 collective-permute-start.16
  124.5 1.7 %collective-permute-done.18 = f32[8,1024]{1,0:T(8,128)S(1)} collective-permute-done((f32[8,1024]{1,0:T(8,128)S(1)}, f32[8,1024]{1,0:T(8,128)S(1)}, u32[]{:S(2)}, u32[]{:S(2)}) %collective-permute-start.18) | collective-permute-done | bytes 32800 | tf_op jit(solution)/shard_map/ppermute | solution.py:316
  126.2 1.6 %collective-permute-done.17 = f32[8,1024]{1,0:T(8,128)S(1)} collective-permute-done((f32[8,1024]{1,0:T(8,128)S(1)}, f32[8,1024]{1,0:T(8,128)S(1)}, u32[]{:S(2)}, u32[]{:S(2)}) %collective-permute-start.17) | collective-permute-done | bytes 32800 | tf_op jit(solution)/shard_map/ppermute | solution.py:316
  127.7 0.0 collective-permute-done.16
  127.8 6.3 %collective-permute-start.19 = (f32[32,1024]{1,0:T(8,128)S(1)}, f32[32,1024]{1,0:T(8,128)S(1)}, u32[]{:S(2)}, u32[]{:S(2)}) collective-permute-start(f32[32,1024]{1,0:T(8,128)S(1)} %pad_maximum_fusion.8), channel_id=1, source_target_pairs={{0,1},{1,0},{2,3},{3,2},{4,5},{5,4},{6,7},{7,6},{8,9},{9,8},{10,11... | collective-permute-start | bytes 393224 | tf_op jit(solution)/shard_map/ppermute | solution.py:316
  134.1 0.6 slice_add_fusion
  134.7 0.3 collective-permute-done.19
  135.1 0.6 slice.145
  135.7 0.7 pad_maximum_fusion.7
  (18 shorter events, 0.4 us)
Async XLA Ops:
  11.4 3.0 %collective-permute-start = (f32[16,16,1024]{2,1,0:T(8,128)S(1)}, f32[16,16,1024]{2,1,0:T(8,128)S(1)}, u32[]{:S(2)}, u32[]{:S(2)}) collective-permute-start(f32[16,16,1024]{2,1,0:T(8,128)S(1)} %get-tuple-element.44), channel_id=1, source_target_pairs={{0,1},{1,0},{2,3},{3,2},{4,5},{5,4},{6,7},{7,6},{8,9},{9,8},{10,11... | collective-permute-start | bytes 3145736 | tf_op jit(solution)/shard_map/ppermute | solution.py:316
  14.1 1.6 %copy-start = (bf16[1024,1024]{1,0:T(8,128)(2,1)S(1)}, bf16[1024,1024]{1,0:T(8,128)(2,1)}, u32[]{:S(2)}) copy-start(bf16[1024,1024]{1,0:T(8,128)(2,1)} %critic_middle_ref.3) | copy-start | bytes 6291460
  14.2 28.6 %collective-permute-start.3 = (f32[16,16,1024]{2,1,0:T(8,128)S(1)}, f32[16,16,1024]{2,1,0:T(8,128)S(1)}, u32[]{:S(2)}, u32[]{:S(2)}) collective-permute-start(f32[16,16,1024]{2,1,0:T(8,128)S(1)} %get-tuple-element.46), channel_id=1, source_target_pairs={{0,1},{1,0},{2,3},{3,2},{4,5},{5,4},{6,7},{7,6},{8,9},{9,8},{10,11... | collective-permute-start | bytes 3145736 | tf_op jit(solution)/shard_map/ppermute | solution.py:316
  19.3 23.3 %collective-permute-start.6 = (f32[32,1024]{1,0:T(8,128)S(1)}, f32[32,1024]{1,0:T(8,128)S(1)}, u32[]{:S(2)}, u32[]{:S(2)}) collective-permute-start(f32[32,1024]{1,0:T(8,128)S(1)} %slice_select_fusion), channel_id=1, source_target_pairs={{0,1},{1,0},{2,3},{3,2},{4,5},{5,4},{6,7},{7,6},{8,9},{9,8},{10,11... | collective-permute-start | bytes 393224 | tf_op jit(solution)/shard_map/ppermute | solution.py:316
  19.6 34.7 %collective-permute-start.1 = (f32[128,1024]{1,0:T(8,128)S(1)}, f32[128,1024]{1,0:T(8,128)S(1)}, u32[]{:S(2)}, u32[]{:S(2)}) collective-permute-start(f32[128,1024]{1,0:T(8,128)S(1)} %bitcast.21), channel_id=1, source_target_pairs={{0,2},{1,3},{2,4},{3,5},{4,6},{5,7},{6,8},{7,9},{8,10},{9,11},{10,... | collective-permute-start | bytes 1572872 | tf_op jit(solution)/shard_map/ppermute | solution.py:313
  21.5 32.7 %collective-permute-start.2 = (f32[128,1024]{1,0:T(8,128)S(1)}, f32[128,1024]{1,0:T(8,128)S(1)}, u32[]{:S(2)}, u32[]{:S(2)}) collective-permute-start(f32[128,1024]{1,0:T(8,128)S(1)} %bitcast.20), channel_id=1, source_target_pairs={{0,62},{1,63},{2,0},{3,1},{4,2},{5,3},{6,4},{7,5},{8,6},{9,7},{10,... | collective-permute-start | bytes 1572872 | tf_op jit(solution)/shard_map/ppermute | solution.py:313
  42.6 15.8 %collective-permute-start.7 = (f32[16,1024]{1,0:T(8,128)S(1)}, f32[16,1024]{1,0:T(8,128)S(1)}, u32[]{:S(2)}, u32[]{:S(2)}) collective-permute-start(f32[16,1024]{1,0:T(8,128)S(1)} %slice_select_fusion.1), channel_id=1, source_target_pairs={{0,2},{1,3},{2,0},{3,1},{4,6},{5,7},{6,4},{7,5},{8,10},{9,11},{10,... | collective-permute-start | bytes 196616 | tf_op jit(solution)/shard_map/ppermute | solution.py:316
  54.6 11.1 %collective-permute-start.4 = (f32[64,1024]{1,0:T(8,128)S(1)}, f32[64,1024]{1,0:T(8,128)S(1)}, u32[]{:S(2)}, u32[]{:S(2)}) collective-permute-start(f32[64,1024]{1,0:T(8,128)S(1)} %get-tuple-element.82), channel_id=1, source_target_pairs={{0,4},{1,5},{2,6},{3,7},{4,8},{5,9},{6,10},{7,11},{8,12},{9,13},{1... | collective-permute-start | bytes 786440 | tf_op jit(solution)/shard_map/ppermute | solution.py:313
  54.8 10.9 %collective-permute-start.5 = (f32[64,1024]{1,0:T(8,128)S(1)}, f32[64,1024]{1,0:T(8,128)S(1)}, u32[]{:S(2)}, u32[]{:S(2)}) collective-permute-start(f32[64,1024]{1,0:T(8,128)S(1)} %get-tuple-element.84), channel_id=1, source_target_pairs={{0,60},{1,61},{2,62},{3,63},{4,0},{5,1},{6,2},{7,3},{8,4},{9,5},{1... | collective-permute-start | bytes 786440 | tf_op jit(solution)/shard_map/ppermute | solution.py:313
  58.5 6.9 %collective-permute-start.8 = (f32[8,1024]{1,0:T(8,128)S(1)}, f32[8,1024]{1,0:T(8,128)S(1)}, u32[]{:S(2)}, u32[]{:S(2)}) collective-permute-start(f32[8,1024]{1,0:T(8,128)S(1)} %slice_select_fusion.2), channel_id=1, source_target_pairs={{0,4},{1,5},{2,6},{3,7},{4,0},{5,1},{6,2},{7,3},{8,12},{9,13},{10,... | collective-permute-start | bytes 98312 | tf_op jit(solution)/shard_map/ppermute | solution.py:316
  65.9 8.3 %collective-permute-start.10 = (f32[24,1024]{1,0:T(8,128)S(1)}, f32[24,1024]{1,0:T(8,128)S(1)}, u32[]{:S(2)}, u32[]{:S(2)}) collective-permute-start(f32[24,1024]{1,0:T(8,128)S(1)} %get-tuple-element.97), channel_id=1, source_target_pairs={{0,56},{1,57},{2,58},{3,59},{4,60},{5,61},{6,62},{7,63},{8,0},{9,1... | collective-permute-start | bytes 294920 | tf_op jit(solution)/shard_map/ppermute | solution.py:313
  69.1 7.7 %collective-permute-start.9 = (f32[24,1024]{1,0:T(8,128)S(1)}, f32[24,1024]{1,0:T(8,128)S(1)}, u32[]{:S(2)}, u32[]{:S(2)}) collective-permute-start(f32[24,1024]{1,0:T(8,128)S(1)} %get-tuple-element.98), channel_id=1, source_target_pairs={{0,8},{1,9},{2,10},{3,11},{4,12},{5,13},{6,14},{7,15},{8,16},{9,17... | collective-permute-start | bytes 294920 | tf_op jit(solution)/shard_map/ppermute | solution.py:313
  76.8 8.6 %collective-permute-start.12 = (f32[24,1024]{1,0:T(8,128)S(1)}, f32[24,1024]{1,0:T(8,128)S(1)}, u32[]{:S(2)}, u32[]{:S(2)}) collective-permute-start(f32[24,1024]{1,0:T(8,128)S(1)} %get-tuple-element.95), channel_id=1, source_target_pairs={{0,56},{1,57},{2,58},{3,59},{4,60},{5,61},{6,62},{7,63},{8,0},{9,1... | collective-permute-start | bytes 294920 | tf_op jit(solution)/shard_map/ppermute | solution.py:313
  80.3 8.4 %collective-permute-start.11 = (f32[24,1024]{1,0:T(8,128)S(1)}, f32[24,1024]{1,0:T(8,128)S(1)}, u32[]{:S(2)}, u32[]{:S(2)}) collective-permute-start(f32[24,1024]{1,0:T(8,128)S(1)} %get-tuple-element.96), channel_id=1, source_target_pairs={{0,8},{1,9},{2,10},{3,11},{4,12},{5,13},{6,14},{7,15},{8,16},{9,17... | collective-permute-start | bytes 294920 | tf_op jit(solution)/shard_map/ppermute | solution.py:313
  88.8 9.0 %collective-permute-start.14 = (f32[24,1024]{1,0:T(8,128)S(1)}, f32[24,1024]{1,0:T(8,128)S(1)}, u32[]{:S(2)}, u32[]{:S(2)}) collective-permute-start(f32[24,1024]{1,0:T(8,128)S(1)} %get-tuple-element.93), channel_id=1, source_target_pairs={{0,56},{1,57},{2,58},{3,59},{4,60},{5,61},{6,62},{7,63},{8,0},{9,1... | collective-permute-start | bytes 294920 | tf_op jit(solution)/shard_map/ppermute | solution.py:313
  92.6 10.4 %collective-permute-start.13 = (f32[24,1024]{1,0:T(8,128)S(1)}, f32[24,1024]{1,0:T(8,128)S(1)}, u32[]{:S(2)}, u32[]{:S(2)}) collective-permute-start(f32[24,1024]{1,0:T(8,128)S(1)} %get-tuple-element.94), channel_id=1, source_target_pairs={{0,8},{1,9},{2,10},{3,11},{4,12},{5,13},{6,14},{7,15},{8,16},{9,17... | collective-permute-start | bytes 294920 | tf_op jit(solution)/shard_map/ppermute | solution.py:313
  103.0 10.6 %collective-permute-start.15 = (f32[24,1024]{1,0:T(8,128)S(1)}, f32[24,1024]{1,0:T(8,128)S(1)}, u32[]{:S(2)}, u32[]{:S(2)}) collective-permute-start(f32[24,1024]{1,0:T(8,128)S(1)} %fusion.7), channel_id=1, source_target_pairs={{0,8},{1,9},{2,10},{3,11},{4,12},{5,13},{6,14},{7,15},{8,16},{9,17... | collective-permute-start | bytes 294920 | tf_op jit(solution)/shard_map/ppermute | solution.py:313
  113.6 12.6 %collective-permute-start.18 = (f32[8,1024]{1,0:T(8,128)S(1)}, f32[8,1024]{1,0:T(8,128)S(1)}, u32[]{:S(2)}, u32[]{:S(2)}) collective-permute-start(f32[8,1024]{1,0:T(8,128)S(1)} %add_add_fusion), channel_id=1, source_target_pairs={{0,6},{1,7},{2,4},{3,5},{4,2},{5,3},{6,0},{7,1},{8,14},{9,15},{10,... | collective-permute-start | bytes 98312 | tf_op jit(solution)/shard_map/ppermute | solution.py:316
  124.1 3.7 %collective-permute-start.17 = (f32[8,1024]{1,0:T(8,128)S(1)}, f32[8,1024]{1,0:T(8,128)S(1)}, u32[]{:S(2)}, u32[]{:S(2)}) collective-permute-start(f32[8,1024]{1,0:T(8,128)S(1)} %add_add_fusion), channel_id=1, source_target_pairs={{0,4},{1,5},{2,6},{3,7},{4,0},{5,1},{6,2},{7,3},{8,12},{9,13},{10,... | collective-permute-start | bytes 98312 | tf_op jit(solution)/shard_map/ppermute | solution.py:316
  124.1 3.7 %collective-permute-start.16 = (f32[8,1024]{1,0:T(8,128)S(1)}, f32[8,1024]{1,0:T(8,128)S(1)}, u32[]{:S(2)}, u32[]{:S(2)}) collective-permute-start(f32[8,1024]{1,0:T(8,128)S(1)} %add_add_fusion), channel_id=1, source_target_pairs={{0,2},{1,3},{2,0},{3,1},{4,6},{5,7},{6,4},{7,5},{8,10},{9,11},{10,... | collective-permute-start | bytes 98312 | tf_op jit(solution)/shard_map/ppermute | solution.py:316
  127.8 7.3 %collective-permute-start.19 = (f32[32,1024]{1,0:T(8,128)S(1)}, f32[32,1024]{1,0:T(8,128)S(1)}, u32[]{:S(2)}, u32[]{:S(2)}) collective-permute-start(f32[32,1024]{1,0:T(8,128)S(1)} %pad_maximum_fusion.8), channel_id=1, source_target_pairs={{0,1},{1,0},{2,3},{3,2},{4,5},{5,4},{6,7},{7,6},{8,9},{9,8},{10,11... | collective-permute-start | bytes 393224 | tf_op jit(solution)/shard_map/ppermute | solution.py:316
where the time goes:
time: 138 us; the launch traced here: 136 us
  starting transfers between devices  64.4 us (47%)
  waiting for transfers between devices  50.8 us (37%)
  Pallas kernels  16.3 us (12%)
  other arithmetic  2.15 us (2%)
  local copies, waits for them, and re-layouts  1.88 us (1%)
    ppermute x11, starting transfers between devices, shift(): return lax.ppermute(x, 'env', pairs)  45.7 us
    ppermute x11, waiting for transfers between devices, shift(): return lax.ppermute(x, 'env', pairs)  40.5 us
    ppermute x9, starting transfers between devices, swap(): return lax.ppermute(x, 'env', [(e, e ^ mask) for e in range(devices)])  18.7 us
    pallas_call x1, Pallas kernels, local_window(): pl.pallas_call(functools.partial(window_kernel, loss_scale), in_specs=[sm...  10.8 us
    ppermute x9, waiting for transfers between devices, swap(): return lax.ppermute(x, 'env', [(e, e ^ mask) for e in range(devices)])  10.3 us
    pallas_call x1, Pallas kernels, small_gradients(): pl.pallas_call(back_kernel, in_specs=[vmem] * 6, out_specs=vmem, out_shap...  3.51 us
  transfers between devices with their start and end apart: 20, of which 13 were waited for; matrix products, arithmetic and copies ran while one was open for 1% of the time, Pallas kernels for 4%

commit v1 on v0

v1 whole, which is shorter than its diff:
```python
import functools
import math

import jax
import jax.numpy as jnp
from jax import lax
from jax.experimental import pallas as pl
from jax.experimental.pallas import tpu as pltpu
from jax.sharding import PartitionSpec as P


TIME_STEP = 0.05
NOISE_UNIT = 0.3 / 32768.0
DISCOUNT = 0.99
TRACE_DECAY = 0.95
LEVELS = 2
CORES = 2

F32 = jnp.float32
BF16 = jnp.bfloat16
NT = (((1,), (1,)), ((), ()))
TN = (((0,), (0,)), ((), ()))


def mm(a, b, dims=(((1,), (0,)), ((), ()))):
    return lax.dot_general(a, b, dims, preferred_element_type=F32)


def distances(ring):
    far = ring // 2
    return [*range(far, 0, -4), *range(far - 2, 0, -4)], [*range(far - 1, 0, -4)], [*range(far - 3, 0, -4)]


def column(row, lanes):
    return jnp.transpose(jnp.broadcast_to(row, (lanes, row.shape[1])))


def owned_rows(first, delta, owners, size):
    rows = delta.shape[1]
    left = [first[pl.ds(pl.multiple_of(o * size, size), size), :rows] for o in owners]
    return mm(jnp.concatenate(left, axis=0), delta[...], NT)


def spread_gradient(ring, away, first, delta, mine_ref, yours_ref):
    size = mine_ref.shape[0] // len(away)
    index = lax.axis_index("env")
    here, core = index // CORES, lax.rem(index, CORES)
    side = 1 - 2 * core
    for ref, way, serves in ((mine_ref, side, core == 0), (yours_ref, -side, core == 1)):
        part = owned_rows(first, delta, [lax.rem(here + way * o + ring, ring) for o in away], size)
        for i, o in enumerate(away):
            piece = part[i * size : (i + 1) * size]
            if 2 * o == ring:
                piece = jnp.where(serves, piece, 0.0)
            ref[i * size : (i + 1) * size] = piece


def window_kernel(
    loss_scale,
    ring,
    away,
    obs_ref,
    dyn_state_ref,
    dyn_act_ref,
    gain_ref,
    reward_weight_ref,
    contacts_ref,
    noise_ref,
    policy_in_ref,
    policy_out_ref,
    critic_in_ref,
    critic_middle_ref,
    critic_out_ref,
    targets_ref,
    inputs,
    first,
    middle,
    delta,
    weight_rows,
    mine_ref,
    yours_ref,
    state_mix,
    middle_copy,
    middle_t,
    out_col,
    act_cols,
    weight_col,
    arrived,
):
    fetch = pltpu.make_async_copy(critic_middle_ref, middle_copy, arrived)
    fetch.start()
    obs, env = obs_ref.shape
    steps, feet, _ = contacts_ref.shape
    act = dyn_act_ref.shape[0]
    pol = policy_out_ref.shape[1]
    hid = critic_middle_ref.shape[0]
    rows = steps * env
    mixing = jnp.concatenate(
        [jnp.transpose(policy_in_ref[...].astype(F32)), dyn_state_ref[...]]
        + [gain_ref[k] for k in range(feet)],
        axis=0,
    )
    top = mixing.astype(BF16).astype(F32)
    state_mix[...] = jnp.concatenate([top, top, mixing - top], axis=1).astype(BF16)
    for a in range(act):
        act_cols[a] = column(dyn_act_ref[a : a + 1, :], env)
    weight_col[...] = column(reward_weight_ref[...], env)
    heads = critic_out_ref[...].astype(F32)
    for j in range(hid // env):
        out_col[j * env : (j + 1) * env, :] = column(heads[j : j + 1, :], env)

    state = obs_ref[...]
    rewards = []
    for t in range(steps):
        high = state.astype(BF16)
        low = (state - high.astype(F32)).astype(BF16)
        inputs[:, t * env : (t + 1) * env] = high
        mixed = mm(state_mix[...], jnp.concatenate([high, low, high], axis=0))
        hidden = jnp.tanh(mixed[:pol]).astype(BF16)
        noise = noise_ref[:, t, :].astype(F32)
        action = jnp.tanh(mm(policy_out_ref[...], hidden)) + NOISE_UNIT * noise
        drift = jnp.tanh(mixed[pol : pol + obs])
        for k in range(feet):
            start = pol + obs * (k + 1)
            touching = contacts_ref[t, k : k + 1, :].astype(F32)
            drift = drift - mixed[start : start + obs] * touching
        for a in range(act):
            drift = drift + act_cols[a] * action[a : a + 1, :]
        state = state + TIME_STEP * drift
        rewards.append(
            0.5
            - jnp.sum(weight_col[...] * state * state, axis=0, keepdims=True) / obs
            - 0.1 * (jnp.sum(action * action, axis=0, keepdims=True) / act)
        )
    inputs[:, rows:] = state.astype(BF16)
    fetch.wait()
    middle_t[...] = jnp.transpose(middle_copy[...])

    block = 256
    for m in range(hid // block):
        at = slice(m * block, (m + 1) * block)
        pre = mm(critic_in_ref[:, at], inputs[...], TN)
        first[at, :] = jnp.maximum(pre, 0.0).astype(BF16)
    values = jnp.zeros((8, rows + env), F32)
    out_row = jnp.concatenate([heads[j : j + 1, :] for j in range(hid // env)], axis=1)
    out_row = jnp.broadcast_to(out_row, (8, hid)).astype(BF16)
    for m in range(hid // block):
        at = slice(m * block, (m + 1) * block)
        kept = jnp.maximum(mm(middle_t[at, :], first[...]), 0.0).astype(BF16)
        middle[at, :] = kept
        values = values + mm(out_row[:, at], kept)
    value = [values[0:1, t * env : (t + 1) * env] for t in range(steps + 1)]
    target = value[steps]
    weights = [None] * steps
    for t in reversed(range(steps)):
        target = rewards[t] + DISCOUNT * (
            (1.0 - TRACE_DECAY) * value[t + 1] + TRACE_DECAY * target
        )
        targets_ref[t : t + 1, :] = target
        weights[t] = loss_scale * (value[t] - target)
        weight_rows[t : t + 1, :] = weights[t]
    for t in range(steps):
        lanes = slice(t * env, (t + 1) * env)
        scaled = out_col[...] * weights[t]
        delta[:, lanes] = jnp.where(middle[:, lanes] > 0, scaled, 0.0).astype(BF16)

    spread_gradient(ring, away, first, delta, mine_ref, yours_ref)


def odd_kernel(ring, away, first, delta, mine_ref, yours_ref, own_ref):
    spread_gradient(ring, away, first, delta, mine_ref, yours_ref)
    here = lax.axis_index("env") // CORES
    own_ref[...] = owned_rows(first, delta, [here], own_ref.shape[0])


def back_kernel(
    critic_middle_ref, inputs, first, middle, delta, weight_rows, small_ref, first_delta
):
    obs = inputs.shape[0]
    hid, rows = delta.shape
    steps = weight_rows.shape[0]
    block = 256
    for m in range(hid // block):
        at = slice(m * block, (m + 1) * block)
        back = mm(critic_middle_ref[at, :], delta[...])
        first_delta[at, :] = jnp.where(first[at, :rows] > 0, back, 0.0).astype(BF16)
    small_ref[...] = jnp.zeros_like(small_ref)
    small_ref[:obs, :] = mm(inputs[:, :rows], first_delta[...], NT)
    weight_row = jnp.concatenate([weight_rows[t : t + 1, :] for t in range(steps)], axis=1)
    weight_high = weight_row.astype(BF16)
    weight_low = (weight_row - weight_high.astype(F32)).astype(BF16)
    both = mm(jnp.concatenate([weight_high, weight_low], axis=0), middle[:, :rows], NT)
    small_ref[obs : obs + 1, :] = both[0:1] + both[1:2]


def local_window(args, devices, small_rows):
    (first_obs, dyn_state, dyn_act, contact_gain, reward_weight, contacts, action_noise,
     policy_in, policy_out, critic_in, critic_middle, critic_out) = args
    obs, env = first_obs.shape
    steps, feet = contacts.shape[:2]
    hid = critic_middle.shape[0]
    pol = policy_out.shape[1]
    rows = steps * env
    act = dyn_act.shape[1]
    loss_scale = math.sqrt(hid) / (rows * devices)
    ring = devices // CORES
    size = hid // ring
    even, *odd = distances(ring)
    odd = sum(odd, [])
    vmem = pl.BlockSpec(memory_space=pltpu.VMEM)
    anywhere = pl.BlockSpec(memory_space=pl.ANY)

    def far(x):
        return pltpu.with_memory_space_constraint(x, pltpu.MemorySpace.HBM)

    targets, inputs, first, middle, delta, weight_rows, *near = pl.pallas_call(
        functools.partial(window_kernel, loss_scale, ring, even),
        in_specs=[vmem] * 10 + [anywhere, vmem],
        out_specs=[vmem] * 8,
        out_shape=[
            jax.ShapeDtypeStruct((steps, env), F32),
            pltpu.VMEM((obs, rows + env), BF16),
            pltpu.VMEM((hid, rows + env), BF16),
            pltpu.VMEM((hid, rows + env), BF16),
            pltpu.VMEM((hid, rows), BF16),
            pltpu.VMEM((steps, env), F32),
            pltpu.VMEM((len(even) * size, hid), F32),
            pltpu.VMEM((len(even) * size, hid), F32),
        ],
        scratch_shapes=[
            pltpu.VMEM((pol + obs * (feet + 1), 3 * obs), BF16),
            pltpu.VMEM((hid, hid), BF16),
            pltpu.VMEM((hid, hid), BF16),
            pltpu.VMEM((hid, env), F32),
            pltpu.VMEM((act, obs, env), F32),
            pltpu.VMEM((obs, env), F32),
            pltpu.SemaphoreType.DMA(()),
        ],
        compiler_params=pltpu.CompilerParams(vmem_limit_bytes=24 * 2**20),
    )(
        *(
            far(x)
            for x in (
                first_obs, dyn_state, dyn_act.T, contact_gain, reward_weight[None, :], contacts,
                action_noise.transpose(1, 0, 2), policy_in.T, policy_out, critic_in,
                critic_middle, critic_out.reshape(-1, env),
            )
        )
    )
    small = pl.pallas_call(
        back_kernel,
        in_specs=[vmem] * 6,
        out_specs=vmem,
        out_shape=pltpu.VMEM((small_rows, hid), F32),
        scratch_shapes=[pltpu.VMEM((hid, rows), BF16)],
        compiler_params=pltpu.CompilerParams(vmem_limit_bytes=12 * 2**20),
        cost_estimate=pl.CostEstimate(
            flops=2 * rows * hid * (hid + 2 * obs), bytes_accessed=0, transcendentals=0
        ),
    )(critic_middle, inputs, first, middle, delta, weight_rows)
    other = pl.pallas_call(
        functools.partial(odd_kernel, ring, odd),
        in_specs=[vmem] * 2,
        out_specs=[vmem] * 3,
        out_shape=[
            pltpu.VMEM((len(odd) * size, hid), F32),
            pltpu.VMEM((len(odd) * size, hid), F32),
            pltpu.VMEM((size, hid), F32),
        ],
        compiler_params=pltpu.CompilerParams(vmem_limit_bytes=12 * 2**20),
        cost_estimate=pl.CostEstimate(flops=rows * hid * hid, bytes_accessed=0, transcendentals=0),
    )(first, delta)
    return targets, near, other, small


def reduced_window(*args):
    devices = lax.axis_size("env")
    ring = devices // CORES
    index = lax.axis_index("env")
    obs = args[0].shape[0]
    hid = args[10].shape[0]
    size = hid // ring
    small_rows = 8 * CORES * 2**LEVELS

    bits = [2**k for k in range(LEVELS + 1)]
    held = lax.optimization_barrier((args[0], *(lax.bitwise_and(index, b) != 0 for b in bits)))
    args = (held[0],) + args[1:]
    flags = dict(zip(bits, held[1:]))
    targets, near, other, small = local_window(args, devices, small_rows)

    def onward(x, d):
        pairs = [
            (z * CORES + c, (z + (d if c == 0 else -d)) % ring * CORES + c)
            for z in range(ring)
            for c in range(CORES)
        ]
        return lax.ppermute(x, "env", pairs)

    def swap(x, mask):
        return lax.ppermute(x, "env", [(e, e ^ mask) for e in range(devices)])

    def halves(x, bit):
        half = x.shape[0] // 2
        low, high = x[:half], x[half:]
        return jnp.where(flags[bit], high, low), jnp.where(flags[bit], low, high)

    def joined(mine, other, bit):
        low, high = jnp.where(flags[bit], other, mine), jnp.where(flags[bit], mine, other)
        return jnp.concatenate([low, high], axis=0)

    def folded(x, bit):
        kept, given = halves(x, bit)
        return kept + swap(given, bit)

    got = swap(near[1], 1)
    message = near[0] + got
    got = onward(message, 1)
    rest = other[0] + swap(other[1], 1)
    small = folded(folded(folded(small, 1), CORES), 2 * CORES)
    own = joined(small, swap(small, 1), 1)
    got, rest, own = lax.optimization_barrier((got, rest, own))
    half = rest.shape[0] // 2
    message, kept = rest[:half] + got[:half], rest[half:] + got[half:]
    got, passed = lax.optimization_barrier((onward(message, 2), onward(own, 4)))
    kept = kept + got

    hops = kept.shape[0] // size
    chunk = kept[:size]
    sums = [passed]
    for k in range(1, hops):
        got = onward(jnp.concatenate([chunk, sums[-1] + own], axis=0), 4)
        chunk = got[:size] + kept[k * size : (k + 1) * size]
        sums.append(got[size:])

    side = jnp.where(flags[1], sums[-2], sums[-1])
    small = own + side + swap(side, 1)
    small, _ = halves(small, 1)
    masks = range(1, 2**LEVELS)
    chunk, *parts = lax.optimization_barrier(
        (onward(chunk, 1), *(swap(small, CORES * m) for m in masks))
    )
    parts = [small] + parts
    for level in reversed(range(LEVELS)):
        parts = [joined(parts[m], parts[m + 2**level], CORES * 2**level) for m in range(2**level)]
    small = joined(parts[0], swap(parts[0], 1), 1)
    grad_middle = folded(chunk + other[2], 1)
    return targets, grad_middle, small[:obs], small[obs]


def solution(mesh):
    split = ("parts", "env")
    return jax.shard_map(
        reduced_window,
        mesh=mesh,
        in_specs=(
            P(None, split),
            P(),
            P(),
            P(),
            P(),
            P(None, None, split),
            P(None, None, split),
            P(),
            P(),
            P(),
            P(),
            P(),
        ),
        out_specs=(P(None, split), P(split, None), P("parts", None), P("parts")),
        check_vma=False,
    )
```

time: 138 us -> 130 us (0.942)
  the two profiles are of different devices: /device:TPU:47 before, /device:TPU:37 now
where the time goes in v1:
time: 130 us
  waiting for transfers between devices  69.4 us (53%)
  starting transfers between devices  40.6 us (31%)
  Pallas kernels  16.5 us (13%)
  other arithmetic  2.18 us (2%)
    ppermute x7, waiting for transfers between devices, onward(): return lax.ppermute(x, 'env', pairs)  51.8 us
    ppermute x12, starting transfers between devices, swap(): return lax.ppermute(x, 'env', [(e, e ^ mask) for e in range(devices)])  25.9 us
    ppermute x12, waiting for transfers between devices, swap(): return lax.ppermute(x, 'env', [(e, e ^ mask) for e in range(devices)])  17.5 us
    ppermute x7, starting transfers between devices, onward(): return lax.ppermute(x, 'env', pairs)  14.7 us
    pallas_call x1, Pallas kernels, local_window(): pl.pallas_call(functools.partial(window_kernel, loss_scale, ring, even),...  11.2 us
    pallas_call x1, Pallas kernels, local_window(): pl.pallas_call(back_kernel, in_specs=[vmem] * 6, out_specs=vmem, out_shap...  3.51 us
  transfers between devices with their start and end apart: 19, of which 10 were waited for; matrix products, arithmetic and copies ran while one was open for 1% of the time, Pallas kernels for 4%

profile of v1, /device:TPU:37, one launch (start us, length us, event | category | flops | bytes accessed | tf_op | source)
XLA Modules:
  0.0 130.2 jit_solution(13170065482551778356)
XLA Ops:
  0.6 0.0 copy-start
  0.7 11.2 %shard_map.147 = (f32[8,128]{1,0:T(8,128)}, bf16[48,1152]{1,0:T(8,128)(2,1)S(1)}, bf16[1024,1152]{1,0:T(8,128)(2,1)S(1)}, bf16[1024,1152]{1,0:T(8,128)(2,1)S(1)}...) custom-call(f32[48,128]{1,0:T(8,128)} %obs_ref, ...), custom_call_target="tpu_custom_call" | custom-call | tf_op jit(solution)/shard_map/pallas_call | solution.py:216
  11.9 20.5 %collective-permute-start = (f32[256,1024]{1,0:T(8,128)S(1)}, f32[256,1024]{1,0:T(8,128)S(1)}, u32[]{:S(2)}, u32[]{:S(2)}) collective-permute-start(f32[256,1024]{1,0:T(8,128)S(1)} %get-tuple-element.32), channel_id=1, source_target_pairs={{0,1},{1,0},{2,3},{3,2},{4,5},{5,4},{6,7},{7,6},{8,9},{9,8},{10,11... | collective-permute-start | bytes 3145736 | tf_op jit(solution)/shard_map/ppermute | solution.py:300
  32.4 0.0 copy-done
  32.4 3.5 %shard_map.149 = f32[64,1024]{1,0:T(8,128)S(1)} custom-call(bf16[1024,1024]{1,0:T(8,128)(2,1)S(1)} %copy-done, bf16[48,1152]{1,0:T(8,128)(2,1)S(1)} %get-tuple-element.39.inputs, bf16[1024,1152]{1,0:T(8,128)(2,1)S(1)} %get-tuple-element.33.first, bf16[1024,1152]{1,0:T(8,128)(2,1)S(1)} %get-tuple-element.40.middle, ...), custom_call_target="tpu_custom_call" | custom-call | flops 2348810240 | tf_op jit(solution)/shard_map/pallas_call | solution.py:250
  36.0 0.2 collective-permute-start.3
  36.2 1.3 %collective-permute-done.3 = f32[32,1024]{1,0:T(8,128)S(1)} collective-permute-done((f32[32,1024]{1,0:T(8,128)S(1)}, f32[32,1024]{1,0:T(8,128)S(1)}, u32[]{:S(2)}, u32[]{:S(2)}) %collective-permute-start.3) | collective-permute-done | bytes 131104 | tf_op jit(solution)/shard_map/ppermute | solution.py:300
  37.5 0.3 collective-permute-start.4
  37.8 1.8 %shard_map.148 = (f32[256,1024]{1,0:T(8,128)S(1)}, f32[256,1024]{1,0:T(8,128)S(1)}, f32[32,1024]{1,0:T(8,128)S(1)}) custom-call(bf16[1024,1152]{1,0:T(8,128)(2,1)S(1)} %get-tuple-element.33.first, bf16[1024,1024]{1,0:T(8,128)(2,1)S(1)} %get-tuple-element.34.delta), custom_call_target="tpu_custom_call" | custom-call | flops 1073741824 | tf_op jit(solution)/shard_map/pallas_call | solution.py:261
  39.7 0.2 collective-permute-start.2
  39.8 0.0 collective-permute-done
  39.8 0.2 add.54
  40.0 4.7 %collective-permute-start.1 = (f32[256,1024]{1,0:T(8,128)S(1)}, f32[256,1024]{1,0:T(8,128)S(1)}, u32[]{:S(2)}, u32[]{:S(2)}) collective-permute-start(f32[256,1024]{1,0:T(8,128)S(1)} %add.54), channel_id=1, source_target_pairs={{0,2},{1,63},{2,4},{3,1},{4,6},{5,3},{6,8},{7,5},{8,10},{9,7},{10,... | collective-permute-start | bytes 3145736 | tf_op jit(solution)/shard_map/ppermute | solution.py:297
  44.7 0.0 collective-permute-done.4
  44.7 0.1 collective-permute-start.5
  44.8 12.1 %collective-permute-done.5 = f32[8,1024]{1,0:T(8,128)S(1)} collective-permute-done((f32[8,1024]{1,0:T(8,128)S(1)}, f32[8,1024]{1,0:T(8,128)S(1)}, u32[]{:S(2)}, u32[]{:S(2)}) %collective-permute-start.5) | collective-permute-done | bytes 32800 | tf_op jit(solution)/shard_map/ppermute | solution.py:300
  56.9 0.0 collective-permute-start.6
  56.9 1.2 collective-permute-done.6
  58.1 0.0 collective-permute-done.2
  58.1 0.2 add.55
  58.3 0.0 collective-permute-done.1
  58.3 0.1 slice_add_fusion
  58.4 3.7 %collective-permute-start.7 = (f32[128,1024]{1,0:T(8,128)S(1)}, f32[128,1024]{1,0:T(8,128)S(1)}, u32[]{:S(2)}, u32[]{:S(2)}) collective-permute-start(f32[128,1024]{1,0:T(8,128)S(1)} %slice_add_fusion), channel_id=1, source_target_pairs={{0,4},{1,61},{2,6},{3,63},{4,8},{5,1},{6,10},{7,3},{8,12},{9,5},{1... | collective-permute-start | bytes 1572872 | tf_op jit(solution)/shard_map/ppermute | solution.py:297
  62.1 2.5 %collective-permute-start.8 = (f32[16,1024]{1,0:T(8,128)S(1)}, f32[16,1024]{1,0:T(8,128)S(1)}, u32[]{:S(2)}, u32[]{:S(2)}) collective-permute-start(f32[16,1024]{1,0:T(8,128)S(1)} %pad_maximum_fusion.5), channel_id=1, source_target_pairs={{0,8},{1,57},{2,10},{3,59},{4,12},{5,61},{6,14},{7,63},{8,16},{9,1... | collective-permute-start | bytes 196616 | tf_op jit(solution)/shard_map/ppermute | solution.py:297
  64.6 13.1 %collective-permute-done.8 = f32[16,1024]{1,0:T(8,128)S(1)} collective-permute-done((f32[16,1024]{1,0:T(8,128)S(1)}, f32[16,1024]{1,0:T(8,128)S(1)}, u32[]{:S(2)}, u32[]{:S(2)}) %collective-permute-start.8) | collective-permute-done | bytes 65568 | tf_op jit(solution)/shard_map/ppermute | solution.py:297
  77.7 0.0 collective-permute-done.7
  77.7 0.1 add_add_fusion
  77.9 0.1 collective-permute-start.9
  78.0 12.4 %collective-permute-done.9 = f32[48,1024]{1,0:T(8,128)S(1)} collective-permute-done((f32[48,1024]{1,0:T(8,128)S(1)}, f32[48,1024]{1,0:T(8,128)S(1)}, u32[]{:S(2)}, u32[]{:S(2)}) %collective-permute-start.9) | collective-permute-done | bytes 196640 | tf_op jit(solution)/shard_map/ppermute | solution.py:297
  90.5 0.1 collective-permute-start.10
  90.6 12.9 %collective-permute-done.10 = f32[48,1024]{1,0:T(8,128)S(1)} collective-permute-done((f32[48,1024]{1,0:T(8,128)S(1)}, f32[48,1024]{1,0:T(8,128)S(1)}, u32[]{:S(2)}, u32[]{:S(2)}) %collective-permute-start.10) | collective-permute-done | bytes 196640 | tf_op jit(solution)/shard_map/ppermute | solution.py:297
  103.6 0.6 collective-permute-start.11
  104.2 13.4 %collective-permute-done.11 = f32[48,1024]{1,0:T(8,128)S(1)} collective-permute-done((f32[48,1024]{1,0:T(8,128)S(1)}, f32[48,1024]{1,0:T(8,128)S(1)}, u32[]{:S(2)}, u32[]{:S(2)}) %collective-permute-start.11) | collective-permute-done | bytes 196640 | tf_op jit(solution)/shard_map/ppermute | solution.py:297
  117.6 0.1 collective-permute-start.13
  117.7 3.0 %collective-permute-start.12 = (f32[32,1024]{1,0:T(8,128)S(1)}, f32[32,1024]{1,0:T(8,128)S(1)}, u32[]{:S(2)}, u32[]{:S(2)}) collective-permute-start(f32[32,1024]{1,0:T(8,128)S(1)} %slice_add_fusion.1), channel_id=1, source_target_pairs={{0,2},{1,63},{2,4},{3,1},{4,6},{5,3},{6,8},{7,5},{8,10},{9,7},{10,... | collective-permute-start | bytes 393224 | tf_op jit(solution)/shard_map/ppermute | solution.py:297
  120.7 0.0 collective-permute-done.13
  120.8 0.1 collective-permute-start.16
  120.9 1.0 collective-permute-start.15
  121.9 2.5 %collective-permute-start.14 = (f32[8,1024]{1,0:T(8,128)S(1)}, f32[8,1024]{1,0:T(8,128)S(1)}, u32[]{:S(2)}, u32[]{:S(2)}) collective-permute-start(f32[8,1024]{1,0:T(8,128)S(1)} %slice_select_fusion.4), channel_id=1, source_target_pairs={{0,2},{1,3},{2,0},{3,1},{4,6},{5,7},{6,4},{7,5},{8,10},{9,11},{10,... | collective-permute-start | bytes 98312 | tf_op jit(solution)/shard_map/ppermute | solution.py:300
  124.4 1.6 %collective-permute-done.16 = f32[8,1024]{1,0:T(8,128)S(1)} collective-permute-done((f32[8,1024]{1,0:T(8,128)S(1)}, f32[8,1024]{1,0:T(8,128)S(1)}, u32[]{:S(2)}, u32[]{:S(2)}) %collective-permute-start.16) | collective-permute-done | bytes 32800 | tf_op jit(solution)/shard_map/ppermute | solution.py:300
  126.1 0.0 collective-permute-done.15
  126.1 0.7 collective-permute-done.14
  126.8 0.0 collective-permute-done.12
  126.8 0.5 collective-permute-start.17
  127.4 0.2 collective-permute-start.18
  127.6 0.6 collective-permute-done.17
  128.3 0.6 select_add_fusion.1
  128.9 0.0 collective-permute-done.18
  128.9 0.6 slice.124
  129.5 0.7 pad_maximum_fusion
  (27 shorter events, 0.4 us)
Async XLA Ops:
  0.6 31.8 %copy-start = (bf16[1024,1024]{1,0:T(8,128)(2,1)S(1)}, bf16[1024,1024]{1,0:T(8,128)(2,1)}, u32[]{:S(2)}) copy-start(bf16[1024,1024]{1,0:T(8,128)(2,1)} %critic_middle_ref.3) | copy-start | bytes 6291460
  11.9 27.9 %collective-permute-start = (f32[256,1024]{1,0:T(8,128)S(1)}, f32[256,1024]{1,0:T(8,128)S(1)}, u32[]{:S(2)}, u32[]{:S(2)}) collective-permute-start(f32[256,1024]{1,0:T(8,128)S(1)} %get-tuple-element.32), channel_id=1, source_target_pairs={{0,1},{1,0},{2,3},{3,2},{4,5},{5,4},{6,7},{7,6},{8,9},{9,8},{10,11... | collective-permute-start | bytes 3145736 | tf_op jit(solution)/shard_map/ppermute | solution.py:300
  36.0 1.5 %collective-permute-start.3 = (f32[32,1024]{1,0:T(8,128)S(1)}, f32[32,1024]{1,0:T(8,128)S(1)}, u32[]{:S(2)}, u32[]{:S(2)}) collective-permute-start(f32[32,1024]{1,0:T(8,128)S(1)} %slice_select_fusion), channel_id=1, source_target_pairs={{0,1},{1,0},{2,3},{3,2},{4,5},{5,4},{6,7},{7,6},{8,9},{9,8},{10,11... | collective-permute-start | bytes 393224 | tf_op jit(solution)/shard_map/ppermute | solution.py:300
  37.5 7.2 %collective-permute-start.4 = (f32[16,1024]{1,0:T(8,128)S(1)}, f32[16,1024]{1,0:T(8,128)S(1)}, u32[]{:S(2)}, u32[]{:S(2)}) collective-permute-start(f32[16,1024]{1,0:T(8,128)S(1)} %slice_select_fusion.3), channel_id=1, source_target_pairs={{0,2},{1,3},{2,0},{3,1},{4,6},{5,7},{6,4},{7,5},{8,10},{9,11},{10,... | collective-permute-start | bytes 196616 | tf_op jit(solution)/shard_map/ppermute | solution.py:300
  39.7 18.5 %collective-permute-start.2 = (f32[256,1024]{1,0:T(8,128)S(1)}, f32[256,1024]{1,0:T(8,128)S(1)}, u32[]{:S(2)}, u32[]{:S(2)}) collective-permute-start(f32[256,1024]{1,0:T(8,128)S(1)} %get-tuple-element.36), channel_id=1, source_target_pairs={{0,1},{1,0},{2,3},{3,2},{4,5},{5,4},{6,7},{7,6},{8,9},{9,8},{10,11... | collective-permute-start | bytes 3145736 | tf_op jit(solution)/shard_map/ppermute | solution.py:300
  40.0 18.3 %collective-permute-start.1 = (f32[256,1024]{1,0:T(8,128)S(1)}, f32[256,1024]{1,0:T(8,128)S(1)}, u32[]{:S(2)}, u32[]{:S(2)}) collective-permute-start(f32[256,1024]{1,0:T(8,128)S(1)} %add.54), channel_id=1, source_target_pairs={{0,2},{1,63},{2,4},{3,1},{4,6},{5,3},{6,8},{7,5},{8,10},{9,7},{10,... | collective-permute-start | bytes 3145736 | tf_op jit(solution)/shard_map/ppermute | solution.py:297
  44.7 12.2 %collective-permute-start.5 = (f32[8,1024]{1,0:T(8,128)S(1)}, f32[8,1024]{1,0:T(8,128)S(1)}, u32[]{:S(2)}, u32[]{:S(2)}) collective-permute-start(f32[8,1024]{1,0:T(8,128)S(1)} %slice_select_fusion.5), channel_id=1, source_target_pairs={{0,4},{1,5},{2,6},{3,7},{4,0},{5,1},{6,2},{7,3},{8,12},{9,13},{10,... | collective-permute-start | bytes 98312 | tf_op jit(solution)/shard_map/ppermute | solution.py:300
  56.9 1.2 collective-permute-start.6
  58.4 19.3 %collective-permute-start.7 = (f32[128,1024]{1,0:T(8,128)S(1)}, f32[128,1024]{1,0:T(8,128)S(1)}, u32[]{:S(2)}, u32[]{:S(2)}) collective-permute-start(f32[128,1024]{1,0:T(8,128)S(1)} %slice_add_fusion), channel_id=1, source_target_pairs={{0,4},{1,61},{2,6},{3,63},{4,8},{5,1},{6,10},{7,3},{8,12},{9,5},{1... | collective-permute-start | bytes 1572872 | tf_op jit(solution)/shard_map/ppermute | solution.py:297
  62.1 15.6 %collective-permute-start.8 = (f32[16,1024]{1,0:T(8,128)S(1)}, f32[16,1024]{1,0:T(8,128)S(1)}, u32[]{:S(2)}, u32[]{:S(2)}) collective-permute-start(f32[16,1024]{1,0:T(8,128)S(1)} %pad_maximum_fusion.5), channel_id=1, source_target_pairs={{0,8},{1,57},{2,10},{3,59},{4,12},{5,61},{6,14},{7,63},{8,16},{9,1... | collective-permute-start | bytes 196616 | tf_op jit(solution)/shard_map/ppermute | solution.py:297
  77.9 12.5 %collective-permute-start.9 = (f32[48,1024]{1,0:T(8,128)S(1)}, f32[48,1024]{1,0:T(8,128)S(1)}, u32[]{:S(2)}, u32[]{:S(2)}) collective-permute-start(f32[48,1024]{1,0:T(8,128)S(1)} %pad_maximum_fusion.1), channel_id=1, source_target_pairs={{0,8},{1,57},{2,10},{3,59},{4,12},{5,61},{6,14},{7,63},{8,16},{9,1... | collective-permute-start | bytes 589832 | tf_op jit(solution)/shard_map/ppermute | solution.py:297
  90.5 13.1 %collective-permute-start.10 = (f32[48,1024]{1,0:T(8,128)S(1)}, f32[48,1024]{1,0:T(8,128)S(1)}, u32[]{:S(2)}, u32[]{:S(2)}) collective-permute-start(f32[48,1024]{1,0:T(8,128)S(1)} %pad_maximum_fusion.2), channel_id=1, source_target_pairs={{0,8},{1,57},{2,10},{3,59},{4,12},{5,61},{6,14},{7,63},{8,16},{9,1... | collective-permute-start | bytes 589832 | tf_op jit(solution)/shard_map/ppermute | solution.py:297
  103.6 14.0 %collective-permute-start.11 = (f32[48,1024]{1,0:T(8,128)S(1)}, f32[48,1024]{1,0:T(8,128)S(1)}, u32[]{:S(2)}, u32[]{:S(2)}) collective-permute-start(f32[48,1024]{1,0:T(8,128)S(1)} %pad_maximum_fusion.3), channel_id=1, source_target_pairs={{0,8},{1,57},{2,10},{3,59},{4,12},{5,61},{6,14},{7,63},{8,16},{9,1... | collective-permute-start | bytes 589832 | tf_op jit(solution)/shard_map/ppermute | solution.py:297
  117.6 3.2 %collective-permute-start.13 = (f32[16,1024]{1,0:T(8,128)S(1)}, f32[16,1024]{1,0:T(8,128)S(1)}, u32[]{:S(2)}, u32[]{:S(2)}) collective-permute-start(f32[16,1024]{1,0:T(8,128)S(1)} %slice_select_fusion.1), channel_id=1, source_target_pairs={{0,1},{1,0},{2,3},{3,2},{4,5},{5,4},{6,7},{7,6},{8,9},{9,8},{10,11... | collective-permute-start | bytes 196616 | tf_op jit(solution)/shard_map/ppermute | solution.py:300
  117.7 9.0 %collective-permute-start.12 = (f32[32,1024]{1,0:T(8,128)S(1)}, f32[32,1024]{1,0:T(8,128)S(1)}, u32[]{:S(2)}, u32[]{:S(2)}) collective-permute-start(f32[32,1024]{1,0:T(8,128)S(1)} %slice_add_fusion.1), channel_id=1, source_target_pairs={{0,2},{1,63},{2,4},{3,1},{4,6},{5,3},{6,8},{7,5},{8,10},{9,7},{10,... | collective-permute-start | bytes 393224 | tf_op jit(solution)/shard_map/ppermute | solution.py:297
  120.8 5.3 %collective-permute-start.16 = (f32[8,1024]{1,0:T(8,128)S(1)}, f32[8,1024]{1,0:T(8,128)S(1)}, u32[]{:S(2)}, u32[]{:S(2)}) collective-permute-start(f32[8,1024]{1,0:T(8,128)S(1)} %slice_select_fusion.4), channel_id=1, source_target_pairs={{0,6},{1,7},{2,4},{3,5},{4,2},{5,3},{6,0},{7,1},{8,14},{9,15},{10,... | collective-permute-start | bytes 98312 | tf_op jit(solution)/shard_map/ppermute | solution.py:300
  120.9 5.2 %collective-permute-start.15 = (f32[8,1024]{1,0:T(8,128)S(1)}, f32[8,1024]{1,0:T(8,128)S(1)}, u32[]{:S(2)}, u32[]{:S(2)}) collective-permute-start(f32[8,1024]{1,0:T(8,128)S(1)} %slice_select_fusion.4), channel_id=1, source_target_pairs={{0,4},{1,5},{2,6},{3,7},{4,0},{5,1},{6,2},{7,3},{8,12},{9,13},{10,... | collective-permute-start | bytes 98312 | tf_op jit(solution)/shard_map/ppermute | solution.py:300
  121.9 4.8 %collective-permute-start.14 = (f32[8,1024]{1,0:T(8,128)S(1)}, f32[8,1024]{1,0:T(8,128)S(1)}, u32[]{:S(2)}, u32[]{:S(2)}) collective-permute-start(f32[8,1024]{1,0:T(8,128)S(1)} %slice_select_fusion.4), channel_id=1, source_target_pairs={{0,2},{1,3},{2,0},{3,1},{4,6},{5,7},{6,4},{7,5},{8,10},{9,11},{10,... | collective-permute-start | bytes 98312 | tf_op jit(solution)/shard_map/ppermute | solution.py:300
  126.8 1.4 %collective-permute-start.17 = (f32[16,1024]{1,0:T(8,128)S(1)}, f32[16,1024]{1,0:T(8,128)S(1)}, u32[]{:S(2)}, u32[]{:S(2)}) collective-permute-start(f32[16,1024]{1,0:T(8,128)S(1)} %slice_select_fusion.2), channel_id=1, source_target_pairs={{0,1},{1,0},{2,3},{3,2},{4,5},{5,4},{6,7},{7,6},{8,9},{9,8},{10,11... | collective-permute-start | bytes 196616 | tf_op jit(solution)/shard_map/ppermute | solution.py:300
  127.4 1.5 %collective-permute-start.18 = (f32[32,1024]{1,0:T(8,128)S(1)}, f32[32,1024]{1,0:T(8,128)S(1)}, u32[]{:S(2)}, u32[]{:S(2)}) collective-permute-start(f32[32,1024]{1,0:T(8,128)S(1)} %pad_maximum_fusion.4), channel_id=1, source_target_pairs={{0,1},{1,0},{2,3},{3,2},{4,5},{5,4},{6,7},{7,6},{8,9},{9,8},{10,11... | collective-permute-start | bytes 393224 | tf_op jit(solution)/shard_map/ppermute | solution.py:300

commit v2 on v1

--- a/solution.py
+++ b/solution.py
@@ -167,7 +167,8 @@
     spread_gradient(ring, away, first, delta, mine_ref, yours_ref)
 
 
-def odd_kernel(ring, away, first, delta, mine_ref, yours_ref, own_ref):
+def odd_kernel(ring, away, first, delta, targets, mine_ref, yours_ref, own_ref, targets_ref):
+    targets_ref[...] = targets[...]
     spread_gradient(ring, away, first, delta, mine_ref, yours_ref)
     here = lax.axis_index("env") // CORES
     own_ref[...] = owned_rows(first, delta, [here], own_ref.shape[0])
@@ -193,6 +194,22 @@
     small_ref[obs : obs + 1, :] = both[0:1] + both[1:2]
 
 
+def join_kernel(kept, given, mine, yours, grad_middle, grad_in, grad_out):
+    grad_middle[...] = kept[...] + given[...]
+    behind = lax.rem(lax.axis_index("env"), CORES) == 1
+    half = mine.shape[0] // 2
+    obs = grad_in.shape[0]
+    for k in range(2):
+        at = slice(k * half, (k + 1) * half)
+        for c, same in enumerate((jnp.logical_not(behind), behind)):
+            start = (2 * k + c) * half
+            part = jnp.where(same, mine[at, :], yours[at, :])
+            if start + half <= obs:
+                grad_in[start : start + half, :] = part
+            elif start <= obs:
+                grad_out[...] = part[obs - start : obs - start + 1, :]
+
+
 def local_window(args, devices, small_rows):
     (first_obs, dyn_state, dyn_act, contact_gain, reward_weight, contacts, action_noise,
      policy_in, policy_out, critic_in, critic_middle, critic_out) = args
@@ -218,7 +235,7 @@
         in_specs=[vmem] * 10 + [anywhere, vmem],
         out_specs=[vmem] * 8,
         out_shape=[
-            jax.ShapeDtypeStruct((steps, env), F32),
+            pltpu.VMEM((steps, env), F32),
             pltpu.VMEM((obs, rows + env), BF16),
             pltpu.VMEM((hid, rows + env), BF16),
             pltpu.VMEM((hid, rows + env), BF16),
@@ -260,17 +277,18 @@
     )(critic_middle, inputs, first, middle, delta, weight_rows)
     other = pl.pallas_call(
         functools.partial(odd_kernel, ring, odd),
-        in_specs=[vmem] * 2,
-        out_specs=[vmem] * 3,
+        in_specs=[vmem] * 3,
+        out_specs=[vmem] * 4,
         out_shape=[
             pltpu.VMEM((len(odd) * size, hid), F32),
             pltpu.VMEM((len(odd) * size, hid), F32),
             pltpu.VMEM((size, hid), F32),
+            jax.ShapeDtypeStruct((steps, env), F32),
         ],
         compiler_params=pltpu.CompilerParams(vmem_limit_bytes=12 * 2**20),
         cost_estimate=pl.CostEstimate(flops=rows * hid * hid, bytes_accessed=0, transcendentals=0),
-    )(first, delta)
-    return targets, near, other, small
+    )(first, delta, targets)
+    return near, other, small
 
 
 def reduced_window(*args):
@@ -282,11 +300,16 @@
     size = hid // ring
     small_rows = 8 * CORES * 2**LEVELS
 
-    bits = [2**k for k in range(LEVELS + 1)]
-    held = lax.optimization_barrier((args[0], *(lax.bitwise_and(index, b) != 0 for b in bits)))
+    chip_and_core = lax.shift_right_logical(index, 1) + index
+    marks = (
+        lax.bitwise_and(index, 1) != 0,
+        lax.bitwise_and(chip_and_core, 1) != 0,
+        lax.bitwise_and(index, 2 * CORES) != 0,
+    )
+    held = lax.optimization_barrier((args[0], *marks))
     args = (held[0],) + args[1:]
-    flags = dict(zip(bits, held[1:]))
-    targets, near, other, small = local_window(args, devices, small_rows)
+    is_behind, is_odd, is_upper = held[1:]
+    near, (*other, targets), small = local_window(args, devices, small_rows)
 
     def onward(x, d):
         pairs = [
@@ -299,25 +322,29 @@
     def swap(x, mask):
         return lax.ppermute(x, "env", [(e, e ^ mask) for e in range(devices)])
 
-    def halves(x, bit):
+    def across(x):
+        ahead = [(e, (e + 1 if e % CORES else e - 1) % devices) for e in range(devices)]
+        return lax.ppermute(x, "env", ahead)
+
+    def halves(x, upper):
         half = x.shape[0] // 2
         low, high = x[:half], x[half:]
-        return jnp.where(flags[bit], high, low), jnp.where(flags[bit], low, high)
-
-    def joined(mine, other, bit):
-        low, high = jnp.where(flags[bit], other, mine), jnp.where(flags[bit], mine, other)
+        return jnp.where(upper, high, low), jnp.where(upper, low, high)
+
+    def joined(mine, other, upper):
+        low, high = jnp.where(upper, other, mine), jnp.where(upper, mine, other)
         return jnp.concatenate([low, high], axis=0)
 
-    def folded(x, bit):
-        kept, given = halves(x, bit)
-        return kept + swap(given, bit)
-
-    got = swap(near[1], 1)
-    message = near[0] + got
+    message = near[0] + swap(near[1], 1)
+    kept, given = halves(small, is_odd)
     got = onward(message, 1)
+    given = swap(given, 1)
+    kept, given = halves(kept + given, is_behind)
+    given = across(given)
     rest = other[0] + swap(other[1], 1)
-    small = folded(folded(folded(small, 1), CORES), 2 * CORES)
-    own = joined(small, swap(small, 1), 1)
+    kept, given = halves(kept + given, is_upper)
+    small = kept + swap(given, 2 * CORES)
+    own = joined(small, swap(small, 1), is_behind)
     got, rest, own = lax.optimization_barrier((got, rest, own))
     half = rest.shape[0] // 2
     message, kept = rest[:half] + got[:half], rest[half:] + got[half:]
@@ -332,19 +359,28 @@
         chunk = got[:size] + kept[k * size : (k + 1) * size]
         sums.append(got[size:])
 
-    side = jnp.where(flags[1], sums[-2], sums[-1])
-    small = own + side + swap(side, 1)
-    small, _ = halves(small, 1)
-    masks = range(1, 2**LEVELS)
-    chunk, *parts = lax.optimization_barrier(
-        (onward(chunk, 1), *(swap(small, CORES * m) for m in masks))
+    side = jnp.where(is_behind, sums[-2], sums[-1])
+    small, _ = halves(own + side + swap(side, 1), is_behind)
+    chunk = onward(chunk, 1)
+    parts = [small] + [swap(small, CORES * m) for m in range(1, 4)]
+    chunk, *parts = lax.optimization_barrier((chunk, *parts))
+    mine = joined(
+        joined(parts[0], parts[2], is_upper), joined(parts[1], parts[3], is_upper), is_odd
     )
-    parts = [small] + parts
-    for level in reversed(range(LEVELS)):
-        parts = [joined(parts[m], parts[m + 2**level], CORES * 2**level) for m in range(2**level)]
-    small = joined(parts[0], swap(parts[0], 1), 1)
-    grad_middle = folded(chunk + other[2], 1)
-    return targets, grad_middle, small[:obs], small[obs]
+    kept, given = halves(chunk + other[2], is_behind)
+    vmem = pl.BlockSpec(memory_space=pltpu.VMEM)
+    grad_middle, grad_in, grad_out = pl.pallas_call(
+        join_kernel,
+        in_specs=[vmem] * 4,
+        out_specs=[vmem] * 3,
+        out_shape=[
+            jax.ShapeDtypeStruct(kept.shape, F32),
+            jax.ShapeDtypeStruct((obs, hid), F32),
+            jax.ShapeDtypeStruct((1, hid), F32),
+        ],
+        compiler_params=pltpu.CompilerParams(vmem_limit_bytes=4 * 2**20),
+    )(kept, swap(given, 1), mine, swap(mine, 1))
+    return targets, grad_middle, grad_in, grad_out[0]
 
 
 def solution(mesh):

time: 130 us -> 130 us (level)
  the two profiles are of different devices: /device:TPU:37 before, /device:TPU:47 now
where the time goes in v2:
time: 130 us; the launch traced here: 128 us
  starting transfers between devices  69.4 us (53%)
  waiting for transfers between devices  39.9 us (31%)
  Pallas kernels  17.1 us (13%)
    ppermute x11, starting transfers between devices, swap(): return lax.ppermute(x, 'env', [(e, e ^ mask) for e in range(devices)])  43 us
    ppermute x7, waiting for transfers between devices, onward(): return lax.ppermute(x, 'env', pairs)  29.8 us
    ppermute x7, starting transfers between devices, onward(): return lax.ppermute(x, 'env', pairs)  24.2 us
    pallas_call x1, Pallas kernels, local_window(): pl.pallas_call(functools.partial(window_kernel, loss_scale, ring, even),...  10.7 us
    ppermute x11, waiting for transfers between devices, swap(): return lax.ppermute(x, 'env', [(e, e ^ mask) for e in range(devices)])  10.1 us
    pallas_call x1, Pallas kernels, local_window(): pl.pallas_call(back_kernel, in_specs=[vmem] * 6, out_specs=vmem, out_shap...  3.42 us
  transfers between devices with their start and end apart: 19, of which 12 were waited for; matrix products, arithmetic and copies ran while one was open for 0% of the time, Pallas kernels for 4%

profile of v2, /device:TPU:47, one launch (start us, length us, event | category | flops | bytes accessed | tf_op | source)
XLA Modules:
  0.0 128.1 jit_solution(15850813352596230376)
XLA Ops:
  0.6 0.0 copy-start
  0.7 10.7 %shard_map.147 = (f32[8,128]{1,0:T(8,128)S(1)}, bf16[48,1152]{1,0:T(8,128)(2,1)S(1)}, bf16[1024,1152]{1,0:T(8,128)(2,1)S(1)}, bf16[1024,1152]{1,0:T(8,128)(2,1)S...) custom-call(f32[48,128]{1,0:T(8,128)} %obs_ref, ...), custom_call_target="tpu_custom_call" | custom-call | tf_op jit(solution)/shard_map/pallas_call | solution.py:233
  11.4 0.7 collective-permute-start
  12.1 0.0 copy-done
  12.1 3.4 %shard_map.149 = f32[64,1024]{1,0:T(8,128)S(1)} custom-call(bf16[1024,1024]{1,0:T(8,128)(2,1)S(1)} %copy-done, bf16[48,1152]{1,0:T(8,128)(2,1)S(1)} %get-tuple-element.45.inputs, bf16[1024,1152]{1,0:T(8,128)(2,1)S(1)} %get-tuple-element.34.first, bf16[1024,1152]{1,0:T(8,128)(2,1)S(1)} %get-tuple-element.46.middle, ...), custom_call_target="tpu_custom_call" | custom-call | flops 2348810240 | tf_op jit(solution)/shard_map/pallas_call | solution.py:267
  15.6 0.2 collective-permute-start.3
  15.7 1.3 %collective-permute-done.3 = f32[32,1024]{1,0:T(8,128)S(1)} collective-permute-done((f32[32,1024]{1,0:T(8,128)S(1)}, f32[32,1024]{1,0:T(8,128)S(1)}, u32[]{:S(2)}, u32[]{:S(2)}) %collective-permute-start.3) | collective-permute-done | bytes 131104 | tf_op jit(solution)/shard_map/ppermute | solution.py:323
  17.1 2.2 %collective-permute-start.4 = (f32[16,1024]{1,0:T(8,128)S(1)}, f32[16,1024]{1,0:T(8,128)S(1)}, u32[]{:S(2)}, u32[]{:S(2)}) collective-permute-start(f32[16,1024]{1,0:T(8,128)S(1)} %slice_select_fusion.4), channel_id=1, source_target_pairs={{0,63},{1,2},{2,1},{3,4},{4,3},{5,6},{6,5},{7,8},{8,7},{9,10},{10,... | collective-permute-start | bytes 196616 | tf_op jit(solution)/shard_map/ppermute | solution.py:327
  19.3 2.3 %shard_map.148 = (f32[256,1024]{1,0:T(8,128)S(1)}, f32[256,1024]{1,0:T(8,128)S(1)}, f32[32,1024]{1,0:T(8,128)S(1)}, f32[8,128]{1,0:T(8,128)}) custom-call(bf16[1024,1152]{1,0:T(8,128)(2,1)S(1)} %get-tuple-element.34.first, bf16[1024,1024]{1,0:T(8,128)(2,1)S(1)} %get-tuple-element.35.delta, f32[8,128]{1,0:T(8,128)S(1)} %get-tuple-element.36.targets), custom_call_target="tpu_custom_call" | custom-call | flops 1073741824 | tf_op jit(solution)/shard_map/pallas_call | solution.py:278
  21.6 21.3 %collective-permute-start.2 = (f32[256,1024]{1,0:T(8,128)S(1)}, f32[256,1024]{1,0:T(8,128)S(1)}, u32[]{:S(2)}, u32[]{:S(2)}) collective-permute-start(f32[256,1024]{1,0:T(8,128)S(1)} %get-tuple-element.42), channel_id=1, source_target_pairs={{0,1},{1,0},{2,3},{3,2},{4,5},{5,4},{6,7},{7,6},{8,9},{9,8},{10,11... | collective-permute-start | bytes 3145736 | tf_op jit(solution)/shard_map/ppermute | solution.py:323
  42.8 0.0 collective-permute-done
  42.8 0.2 add.55
  43.0 0.6 collective-permute-start.1
  43.6 0.0 collective-permute-done.4
  43.7 0.1 collective-permute-start.5
  43.8 4.3 %collective-permute-done.5 = f32[8,1024]{1,0:T(8,128)S(1)} collective-permute-done((f32[8,1024]{1,0:T(8,128)S(1)}, f32[8,1024]{1,0:T(8,128)S(1)}, u32[]{:S(2)}, u32[]{:S(2)}) %collective-permute-start.5) | collective-permute-done | bytes 32800 | tf_op jit(solution)/shard_map/ppermute | solution.py:323
  48.1 8.1 %collective-permute-start.6 = (f32[8,1024]{1,0:T(8,128)S(1)}, f32[8,1024]{1,0:T(8,128)S(1)}, u32[]{:S(2)}, u32[]{:S(2)}) collective-permute-start(f32[8,1024]{1,0:T(8,128)S(1)} %select_add_fusion.2), channel_id=1, source_target_pairs={{0,1},{1,0},{2,3},{3,2},{4,5},{5,4},{6,7},{7,6},{8,9},{9,8},{10,11... | collective-permute-start | bytes 98312 | tf_op jit(solution)/shard_map/ppermute | solution.py:323
  56.2 0.9 collective-permute-done.6
  57.1 0.0 collective-permute-done.2
  57.1 0.2 add.56
  57.3 0.5 collective-permute-done.1
  57.8 0.1 slice_add_fusion
  57.9 3.7 %collective-permute-start.7 = (f32[128,1024]{1,0:T(8,128)S(1)}, f32[128,1024]{1,0:T(8,128)S(1)}, u32[]{:S(2)}, u32[]{:S(2)}) collective-permute-start(f32[128,1024]{1,0:T(8,128)S(1)} %slice_add_fusion), channel_id=1, source_target_pairs={{0,4},{1,61},{2,6},{3,63},{4,8},{5,1},{6,10},{7,3},{8,12},{9,5},{1... | collective-permute-start | bytes 1572872 | tf_op jit(solution)/shard_map/ppermute | solution.py:320
  61.6 2.5 %collective-permute-start.8 = (f32[16,1024]{1,0:T(8,128)S(1)}, f32[16,1024]{1,0:T(8,128)S(1)}, u32[]{:S(2)}, u32[]{:S(2)}) collective-permute-start(f32[16,1024]{1,0:T(8,128)S(1)} %pad_maximum_fusion.4), channel_id=1, source_target_pairs={{0,8},{1,57},{2,10},{3,59},{4,12},{5,61},{6,14},{7,63},{8,16},{9,1... | collective-permute-start | bytes 196616 | tf_op jit(solution)/shard_map/ppermute | solution.py:320
  64.0 9.4 %collective-permute-done.8 = f32[16,1024]{1,0:T(8,128)S(1)} collective-permute-done((f32[16,1024]{1,0:T(8,128)S(1)}, f32[16,1024]{1,0:T(8,128)S(1)}, u32[]{:S(2)}, u32[]{:S(2)}) %collective-permute-start.8) | collective-permute-done | bytes 65568 | tf_op jit(solution)/shard_map/ppermute | solution.py:320
  73.4 0.0 collective-permute-done.7
  73.4 0.1 add_add_fusion
  73.6 3.6 %collective-permute-start.9 = (f32[48,1024]{1,0:T(8,128)S(1)}, f32[48,1024]{1,0:T(8,128)S(1)}, u32[]{:S(2)}, u32[]{:S(2)}) collective-permute-start(f32[48,1024]{1,0:T(8,128)S(1)} %pad_maximum_fusion), channel_id=1, source_target_pairs={{0,8},{1,57},{2,10},{3,59},{4,12},{5,61},{6,14},{7,63},{8,16},{9,1... | collective-permute-start | bytes 589832 | tf_op jit(solution)/shard_map/ppermute | solution.py:320
  77.2 6.6 %collective-permute-done.9 = f32[48,1024]{1,0:T(8,128)S(1)} collective-permute-done((f32[48,1024]{1,0:T(8,128)S(1)}, f32[48,1024]{1,0:T(8,128)S(1)}, u32[]{:S(2)}, u32[]{:S(2)}) %collective-permute-start.9) | collective-permute-done | bytes 196640 | tf_op jit(solution)/shard_map/ppermute | solution.py:320
  83.9 2.9 %collective-permute-start.10 = (f32[48,1024]{1,0:T(8,128)S(1)}, f32[48,1024]{1,0:T(8,128)S(1)}, u32[]{:S(2)}, u32[]{:S(2)}) collective-permute-start(f32[48,1024]{1,0:T(8,128)S(1)} %pad_maximum_fusion.1), channel_id=1, source_target_pairs={{0,8},{1,57},{2,10},{3,59},{4,12},{5,61},{6,14},{7,63},{8,16},{9,1... | collective-permute-start | bytes 589832 | tf_op jit(solution)/shard_map/ppermute | solution.py:320
  86.7 5.8 %collective-permute-done.10 = f32[48,1024]{1,0:T(8,128)S(1)} collective-permute-done((f32[48,1024]{1,0:T(8,128)S(1)}, f32[48,1024]{1,0:T(8,128)S(1)}, u32[]{:S(2)}, u32[]{:S(2)}) %collective-permute-start.10) | collective-permute-done | bytes 196640 | tf_op jit(solution)/shard_map/ppermute | solution.py:320
  92.6 10.8 %collective-permute-start.11 = (f32[48,1024]{1,0:T(8,128)S(1)}, f32[48,1024]{1,0:T(8,128)S(1)}, u32[]{:S(2)}, u32[]{:S(2)}) collective-permute-start(f32[48,1024]{1,0:T(8,128)S(1)} %pad_maximum_fusion.2), channel_id=1, source_target_pairs={{0,8},{1,57},{2,10},{3,59},{4,12},{5,61},{6,14},{7,63},{8,16},{9,1... | collective-permute-start | bytes 589832 | tf_op jit(solution)/shard_map/ppermute | solution.py:320
  103.4 7.4 %collective-permute-done.11 = f32[48,1024]{1,0:T(8,128)S(1)} collective-permute-done((f32[48,1024]{1,0:T(8,128)S(1)}, f32[48,1024]{1,0:T(8,128)S(1)}, u32[]{:S(2)}, u32[]{:S(2)}) %collective-permute-start.11) | collective-permute-done | bytes 196640 | tf_op jit(solution)/shard_map/ppermute | solution.py:320
  110.8 7.3 %collective-permute-start.13 = (f32[16,1024]{1,0:T(8,128)S(1)}, f32[16,1024]{1,0:T(8,128)S(1)}, u32[]{:S(2)}, u32[]{:S(2)}) collective-permute-start(f32[16,1024]{1,0:T(8,128)S(1)} %slice_select_fusion.1), channel_id=1, source_target_pairs={{0,1},{1,0},{2,3},{3,2},{4,5},{5,4},{6,7},{7,6},{8,9},{9,8},{10,11... | collective-permute-start | bytes 196616 | tf_op jit(solution)/shard_map/ppermute | solution.py:323
  118.1 0.1 collective-permute-start.12
  118.3 0.7 collective-permute-done.13
  119.0 0.1 collective-permute-start.16
  119.2 1.9 %collective-permute-start.15 = (f32[8,1024]{1,0:T(8,128)S(1)}, f32[8,1024]{1,0:T(8,128)S(1)}, u32[]{:S(2)}, u32[]{:S(2)}) collective-permute-start(f32[8,1024]{1,0:T(8,128)S(1)} %slice_select_fusion.5), channel_id=1, source_target_pairs={{0,4},{1,5},{2,6},{3,7},{4,0},{5,1},{6,2},{7,3},{8,12},{9,13},{10,... | collective-permute-start | bytes 98312 | tf_op jit(solution)/shard_map/ppermute | solution.py:323
  121.0 1.7 %collective-permute-start.14 = (f32[8,1024]{1,0:T(8,128)S(1)}, f32[8,1024]{1,0:T(8,128)S(1)}, u32[]{:S(2)}, u32[]{:S(2)}) collective-permute-start(f32[8,1024]{1,0:T(8,128)S(1)} %slice_select_fusion.5), channel_id=1, source_target_pairs={{0,2},{1,3},{2,0},{3,1},{4,6},{5,7},{6,4},{7,5},{8,10},{9,11},{10,... | collective-permute-start | bytes 98312 | tf_op jit(solution)/shard_map/ppermute | solution.py:323
  122.7 1.0 collective-permute-done.16
  123.8 0.0 collective-permute-done.15
  123.8 0.7 collective-permute-done.14
  124.4 0.0 collective-permute-done.12
  124.5 1.5 %collective-permute-start.18 = (f32[32,1024]{1,0:T(8,128)S(1)}, f32[32,1024]{1,0:T(8,128)S(1)}, u32[]{:S(2)}, u32[]{:S(2)}) collective-permute-start(f32[32,1024]{1,0:T(8,128)S(1)} %pad_maximum_fusion.3.mine), channel_id=1, source_target_pairs={{0,1},{1,0},{2,3},{3,2},{4,5},{5,4},{6,7},{7,6},{8,9},{9,8},{10,11... | collective-permute-start | bytes 393224 | tf_op jit(solution)/shard_map/ppermute | solution.py:323
  126.0 0.2 collective-permute-start.17
  126.2 1.2 collective-permute-done.17.given
  127.4 0.0 collective-permute-done.18.yours
  127.4 0.7 shard_map.150
  (26 shorter events, 0.4 us)
Async XLA Ops:
  0.6 11.5 %copy-start = (bf16[1024,1024]{1,0:T(8,128)(2,1)S(1)}, bf16[1024,1024]{1,0:T(8,128)(2,1)}, u32[]{:S(2)}) copy-start(bf16[1024,1024]{1,0:T(8,128)(2,1)} %critic_middle_ref.3) | copy-start | bytes 6291460
  11.4 31.5 %collective-permute-start = (f32[256,1024]{1,0:T(8,128)S(1)}, f32[256,1024]{1,0:T(8,128)S(1)}, u32[]{:S(2)}, u32[]{:S(2)}) collective-permute-start(f32[256,1024]{1,0:T(8,128)S(1)} %get-tuple-element.40), channel_id=1, source_target_pairs={{0,1},{1,0},{2,3},{3,2},{4,5},{5,4},{6,7},{7,6},{8,9},{9,8},{10,11... | collective-permute-start | bytes 3145736 | tf_op jit(solution)/shard_map/ppermute | solution.py:323
  15.6 1.5 %collective-permute-start.3 = (f32[32,1024]{1,0:T(8,128)S(1)}, f32[32,1024]{1,0:T(8,128)S(1)}, u32[]{:S(2)}, u32[]{:S(2)}) collective-permute-start(f32[32,1024]{1,0:T(8,128)S(1)} %slice_select_fusion), channel_id=1, source_target_pairs={{0,1},{1,0},{2,3},{3,2},{4,5},{5,4},{6,7},{7,6},{8,9},{9,8},{10,11... | collective-permute-start | bytes 393224 | tf_op jit(solution)/shard_map/ppermute | solution.py:323
  17.1 26.5 %collective-permute-start.4 = (f32[16,1024]{1,0:T(8,128)S(1)}, f32[16,1024]{1,0:T(8,128)S(1)}, u32[]{:S(2)}, u32[]{:S(2)}) collective-permute-start(f32[16,1024]{1,0:T(8,128)S(1)} %slice_select_fusion.4), channel_id=1, source_target_pairs={{0,63},{1,2},{2,1},{3,4},{4,3},{5,6},{6,5},{7,8},{8,7},{9,10},{10,... | collective-permute-start | bytes 196616 | tf_op jit(solution)/shard_map/ppermute | solution.py:327
  21.6 35.5 %collective-permute-start.2 = (f32[256,1024]{1,0:T(8,128)S(1)}, f32[256,1024]{1,0:T(8,128)S(1)}, u32[]{:S(2)}, u32[]{:S(2)}) collective-permute-start(f32[256,1024]{1,0:T(8,128)S(1)} %get-tuple-element.42), channel_id=1, source_target_pairs={{0,1},{1,0},{2,3},{3,2},{4,5},{5,4},{6,7},{7,6},{8,9},{9,8},{10,11... | collective-permute-start | bytes 3145736 | tf_op jit(solution)/shard_map/ppermute | solution.py:323
  43.0 14.8 %collective-permute-start.1 = (f32[256,1024]{1,0:T(8,128)S(1)}, f32[256,1024]{1,0:T(8,128)S(1)}, u32[]{:S(2)}, u32[]{:S(2)}) collective-permute-start(f32[256,1024]{1,0:T(8,128)S(1)} %add.55), channel_id=1, source_target_pairs={{0,2},{1,63},{2,4},{3,1},{4,6},{5,3},{6,8},{7,5},{8,10},{9,7},{10,... | collective-permute-start | bytes 3145736 | tf_op jit(solution)/shard_map/ppermute | solution.py:320
  43.7 4.4 %collective-permute-start.5 = (f32[8,1024]{1,0:T(8,128)S(1)}, f32[8,1024]{1,0:T(8,128)S(1)}, u32[]{:S(2)}, u32[]{:S(2)}) collective-permute-start(f32[8,1024]{1,0:T(8,128)S(1)} %slice_select_fusion.6), channel_id=1, source_target_pairs={{0,4},{1,5},{2,6},{3,7},{4,0},{5,1},{6,2},{7,3},{8,12},{9,13},{10,... | collective-permute-start | bytes 98312 | tf_op jit(solution)/shard_map/ppermute | solution.py:323
  48.1 9.0 %collective-permute-start.6 = (f32[8,1024]{1,0:T(8,128)S(1)}, f32[8,1024]{1,0:T(8,128)S(1)}, u32[]{:S(2)}, u32[]{:S(2)}) collective-permute-start(f32[8,1024]{1,0:T(8,128)S(1)} %select_add_fusion.2), channel_id=1, source_target_pairs={{0,1},{1,0},{2,3},{3,2},{4,5},{5,4},{6,7},{7,6},{8,9},{9,8},{10,11... | collective-permute-start | bytes 98312 | tf_op jit(solution)/shard_map/ppermute | solution.py:323
  57.9 15.6 %collective-permute-start.7 = (f32[128,1024]{1,0:T(8,128)S(1)}, f32[128,1024]{1,0:T(8,128)S(1)}, u32[]{:S(2)}, u32[]{:S(2)}) collective-permute-start(f32[128,1024]{1,0:T(8,128)S(1)} %slice_add_fusion), channel_id=1, source_target_pairs={{0,4},{1,61},{2,6},{3,63},{4,8},{5,1},{6,10},{7,3},{8,12},{9,5},{1... | collective-permute-start | bytes 1572872 | tf_op jit(solution)/shard_map/ppermute | solution.py:320
  61.6 11.9 %collective-permute-start.8 = (f32[16,1024]{1,0:T(8,128)S(1)}, f32[16,1024]{1,0:T(8,128)S(1)}, u32[]{:S(2)}, u32[]{:S(2)}) collective-permute-start(f32[16,1024]{1,0:T(8,128)S(1)} %pad_maximum_fusion.4), channel_id=1, source_target_pairs={{0,8},{1,57},{2,10},{3,59},{4,12},{5,61},{6,14},{7,63},{8,16},{9,1... | collective-permute-start | bytes 196616 | tf_op jit(solution)/shard_map/ppermute | solution.py:320
  73.6 10.2 %collective-permute-start.9 = (f32[48,1024]{1,0:T(8,128)S(1)}, f32[48,1024]{1,0:T(8,128)S(1)}, u32[]{:S(2)}, u32[]{:S(2)}) collective-permute-start(f32[48,1024]{1,0:T(8,128)S(1)} %pad_maximum_fusion), channel_id=1, source_target_pairs={{0,8},{1,57},{2,10},{3,59},{4,12},{5,61},{6,14},{7,63},{8,16},{9,1... | collective-permute-start | bytes 589832 | tf_op jit(solution)/shard_map/ppermute | solution.py:320
  83.9 8.6 %collective-permute-start.10 = (f32[48,1024]{1,0:T(8,128)S(1)}, f32[48,1024]{1,0:T(8,128)S(1)}, u32[]{:S(2)}, u32[]{:S(2)}) collective-permute-start(f32[48,1024]{1,0:T(8,128)S(1)} %pad_maximum_fusion.1), channel_id=1, source_target_pairs={{0,8},{1,57},{2,10},{3,59},{4,12},{5,61},{6,14},{7,63},{8,16},{9,1... | collective-permute-start | bytes 589832 | tf_op jit(solution)/shard_map/ppermute | solution.py:320
  92.6 18.2 %collective-permute-start.11 = (f32[48,1024]{1,0:T(8,128)S(1)}, f32[48,1024]{1,0:T(8,128)S(1)}, u32[]{:S(2)}, u32[]{:S(2)}) collective-permute-start(f32[48,1024]{1,0:T(8,128)S(1)} %pad_maximum_fusion.2), channel_id=1, source_target_pairs={{0,8},{1,57},{2,10},{3,59},{4,12},{5,61},{6,14},{7,63},{8,16},{9,1... | collective-permute-start | bytes 589832 | tf_op jit(solution)/shard_map/ppermute | solution.py:320
  110.8 8.2 %collective-permute-start.13 = (f32[16,1024]{1,0:T(8,128)S(1)}, f32[16,1024]{1,0:T(8,128)S(1)}, u32[]{:S(2)}, u32[]{:S(2)}) collective-permute-start(f32[16,1024]{1,0:T(8,128)S(1)} %slice_select_fusion.1), channel_id=1, source_target_pairs={{0,1},{1,0},{2,3},{3,2},{4,5},{5,4},{6,7},{7,6},{8,9},{9,8},{10,11... | collective-permute-start | bytes 196616 | tf_op jit(solution)/shard_map/ppermute | solution.py:323
  118.1 6.3 %collective-permute-start.12 = (f32[32,1024]{1,0:T(8,128)S(1)}, f32[32,1024]{1,0:T(8,128)S(1)}, u32[]{:S(2)}, u32[]{:S(2)}) collective-permute-start(f32[32,1024]{1,0:T(8,128)S(1)} %slice_add_fusion.1), channel_id=1, source_target_pairs={{0,2},{1,63},{2,4},{3,1},{4,6},{5,3},{6,8},{7,5},{8,10},{9,7},{10,... | collective-permute-start | bytes 393224 | tf_op jit(solution)/shard_map/ppermute | solution.py:320
  119.0 4.7 %collective-permute-start.16 = (f32[8,1024]{1,0:T(8,128)S(1)}, f32[8,1024]{1,0:T(8,128)S(1)}, u32[]{:S(2)}, u32[]{:S(2)}) collective-permute-start(f32[8,1024]{1,0:T(8,128)S(1)} %slice_select_fusion.5), channel_id=1, source_target_pairs={{0,6},{1,7},{2,4},{3,5},{4,2},{5,3},{6,0},{7,1},{8,14},{9,15},{10,... | collective-permute-start | bytes 98312 | tf_op jit(solution)/shard_map/ppermute | solution.py:323
  119.2 4.6 %collective-permute-start.15 = (f32[8,1024]{1,0:T(8,128)S(1)}, f32[8,1024]{1,0:T(8,128)S(1)}, u32[]{:S(2)}, u32[]{:S(2)}) collective-permute-start(f32[8,1024]{1,0:T(8,128)S(1)} %slice_select_fusion.5), channel_id=1, source_target_pairs={{0,4},{1,5},{2,6},{3,7},{4,0},{5,1},{6,2},{7,3},{8,12},{9,13},{10,... | collective-permute-start | bytes 98312 | tf_op jit(solution)/shard_map/ppermute | solution.py:323
  121.0 3.4 %collective-permute-start.14 = (f32[8,1024]{1,0:T(8,128)S(1)}, f32[8,1024]{1,0:T(8,128)S(1)}, u32[]{:S(2)}, u32[]{:S(2)}) collective-permute-start(f32[8,1024]{1,0:T(8,128)S(1)} %slice_select_fusion.5), channel_id=1, source_target_pairs={{0,2},{1,3},{2,0},{3,1},{4,6},{5,7},{6,4},{7,5},{8,10},{9,11},{10,... | collective-permute-start | bytes 98312 | tf_op jit(solution)/shard_map/ppermute | solution.py:323
  124.5 2.9 %collective-permute-start.18 = (f32[32,1024]{1,0:T(8,128)S(1)}, f32[32,1024]{1,0:T(8,128)S(1)}, u32[]{:S(2)}, u32[]{:S(2)}) collective-permute-start(f32[32,1024]{1,0:T(8,128)S(1)} %pad_maximum_fusion.3.mine), channel_id=1, source_target_pairs={{0,1},{1,0},{2,3},{3,2},{4,5},{5,4},{6,7},{7,6},{8,9},{9,8},{10,11... | collective-permute-start | bytes 393224 | tf_op jit(solution)/shard_map/ppermute | solution.py:323
  126.0 1.4 %collective-permute-start.17 = (f32[16,1024]{1,0:T(8,128)S(1)}, f32[16,1024]{1,0:T(8,128)S(1)}, u32[]{:S(2)}, u32[]{:S(2)}) collective-permute-start(f32[16,1024]{1,0:T(8,128)S(1)} %get-tuple-element.64), channel_id=1, source_target_pairs={{0,1},{1,0},{2,3},{3,2},{4,5},{5,4},{6,7},{7,6},{8,9},{9,8},{10,11... | collective-permute-start | bytes 196616 | tf_op jit(solution)/shard_map/ppermute | solution.py:323
